TPU v7x, 256 devices: a whole 4x4x8 slice. The times are simulated.
256 devices in a mesh: gx: 8 (over z_lo, core), gy: 32 (over z_hi, y, x).
Axes of the slice: x: 4, y: 4, z: 8 (z_hi: 2, z_lo: 4; z = z_hi * 4 + z_lo), core: 2. Of those that a mesh axis runs over, the one named last changes fastest.
Arguments:
- density: float32 [128, 512, 256], P('gx', 'gy'), may hold values from 0.5 to 2
- momentum: float32 [3, 128, 512, 256], P(None, 'gx', 'gy'), may hold values from -3 to 3
- energy: float32 [128, 512, 256], P('gx', 'gy'), may hold values from 1 to 3
- parcel_mass: float32 [2097152], P(('gx', 'gy')), may hold values from 0.2 to 2
- droplet_velocity: float32 [3, 2097152], P(None, ('gx', 'gy')), may hold values from -4 to 4
- parcel_temp: float32 [2097152], P(('gx', 'gy')), may hold values from 0.1 to 4
- parcel_cell: int32 [3, 2097152], P(None, ('gx', 'gy')), may hold values from 0 to 511, as said below
- parcel_count: int32 [256], P(('gx', 'gy')), may hold values from 2048 to 8192, as said below
Outputs:
- updated_fluid_density: float32 [128, 512, 256], P('gx', 'gy')
- updated_fluid_impulse: float32 [3, 128, 512, 256], P(None, 'gx', 'gy')
- energy_out: float32 [128, 512, 256], P('gx', 'gy')
- moved_state: float32 [5, 2621440], P(None, ('gx', 'gy'))
- moved_cell: int32 [3, 2621440], P(None, ('gx', 'gy'))
- time_step: float32 [], replicated
Inputs may be any that keep to these rules, and one draw needn't show every extreme that they name: `parcel_cell`: each row of device d lies in d's block of 16 x 16 x 256 cells or in the layer of cells just beyond one of its four side faces inside the grid, never beyond an edge. Among the live rows of one device at most 512 lie beyond any one face; on every device some face along each of the two axes has exactly 512. `parcel_count`: some devices are full.
All inputs are finite; a program needn't handle non-finite values.
Results may differ from a plain program's by a relative error of at most 0.0003.
Values sent between devices are 32-bit elements; how exact they have to be, the bound alone decides.
A program may use at most 192 MiB of HBM per device.

v0:
```python
import functools

import jax
import jax.numpy as jnp
from jax import lax
from jax.experimental import pallas as pl
from jax.experimental.pallas import tpu as pltpu
from jax.sharding import PartitionSpec as P

ADIABATIC_INDEX = 1.4
KICK = 0.25
COURANT = 0.4
SHRINK = 0.5
MESH = pl.DeviceIdType.MESH
CHUNK = 1024
F32 = jnp.float32
BF16 = jnp.bfloat16
F8 = jnp.float8_e4m3fn
LIFT = 2048.0


def dot_nt(a, b):
    return lax.dot_general(a, b, (((1,), (1,)), ((), ())), preferred_element_type=F32)


def two_terms(x):
    high = x.astype(BF16)
    low = (x - high.astype(F32)).astype(BF16)
    return high, low


def one_hot_rows(row, count):
    lanes = row.shape[1]
    base = (
        jnp.broadcast_to(row, (16, lanes))
        - lax.broadcasted_iota(jnp.int32, (16, lanes), 0).astype(F32)
    ).astype(BF16)
    one, zero = jnp.ones((16, lanes), BF16), jnp.zeros((16, lanes), BF16)
    return jnp.concatenate(
        [jnp.where(base == 16.0 * k, one, zero) for k in range(count // 16)], axis=0
    )


def kernel(
    n_gx, n_gy, count_ref, density_hbm, momentum_hbm, energy_hbm, mass_hbm, vel_hbm, temp_hbm, cell_hbm,
    rho_ref, imp_ref, en_ref, state_ref, moved_ref, step_ref,
    src_ref, pay_ref, col_ref, q_ref, r_ref, a0_ref, a1_ref, b0_ref, b1_ref, c0_ref, c1_ref, d0_ref, d1_ref, acc_ref, low_ref, small_ref,
    out_bucket, in_bucket, out_face, in_face, max_x, max_y,
    bucket_send, bucket_recv, face_send, face_recv, mx_send, mx_recv, my_send, my_recv,
    density_ref, momentum_ref, energy_ref, mass_ref, vel_ref, temp_ref, cell_ref, load_sem,
):
    sources = (mass_hbm, temp_hbm, vel_hbm, cell_hbm, energy_hbm, density_hbm, momentum_hbm)
    places = (mass_ref, temp_ref, vel_ref, cell_ref, energy_ref, density_ref, momentum_ref)
    loads = []
    for k in range(7):
        load = pltpu.make_async_copy(sources[k], places[k], load_sem.at[k])
        load.start()
        loads.append(load)
    gx, gy = lax.axis_index("gx"), lax.axis_index("gy")
    cx, cy, nz = density_ref.shape
    rows = mass_ref.shape[1]
    cap = rows // 16
    per = cap // 128

    barrier = pltpu.get_barrier_semaphore()
    for k in range(1, n_gx):
        pl.semaphore_signal(barrier, inc=1, device_id={"gx": lax.rem(gx + k, n_gx)}, device_id_type=MESH)
    for k in range(1, n_gy):
        pl.semaphore_signal(barrier, inc=1, device_id={"gy": lax.rem(gy + k, n_gy)}, device_id_type=MESH)

    for load in loads[:4]:
        load.wait()
    mass, temp = mass_ref[...], temp_ref[...]
    live = lax.broadcasted_iota(jnp.int32, (1, rows), 1) < count_ref[0]
    evap = jnp.where(live, mass * jax.nn.sigmoid(2.0 * (temp - 2.0)), 0.0)
    vx, vy, vz = vel_ref[0:1, :], vel_ref[1:2, :], vel_ref[2:3, :]
    src_ref[0:1, :] = evap
    src_ref[1:2, :] = evap * vx
    src_ref[2:3, :] = evap * vy
    src_ref[3:4, :] = evap * vz
    src_ref[4:5, :] = evap * (temp + 0.5 * (vx * vx + vy * vy + vz * vz))
    pay_ref[0:1, :] = mass - SHRINK * evap
    pay_ref[1:4, :] = vel_ref[...]
    pay_ref[4:5, :] = temp
    pay_ref[5:8, :] = cell_ref[...].astype(F32)
    lx = cell_ref[0:1, :] - gx * cx
    ly = cell_ref[1:2, :] - gy * cy
    heading = jnp.where(
        lx < 0, 0, jnp.where(lx >= cx, 1, jnp.where(ly < 0, 2, jnp.where(ly >= cy, 3, 4)))
    )
    heading = jnp.where(live, heading, 5)
    stays = heading == 4
    col_ref[...] = jnp.where(stays, lx * cy + ly, -1000).astype(F32)
    state_ref[:, :rows] = jnp.where(stays, pay_ref[0:5, :], 0.0)
    moved_ref[:, :rows] = jnp.where(stays, cell_ref[...], 0)

    blocks = rows // 128
    marks = jnp.where(
        jnp.broadcast_to(heading, (8, rows)) == lax.broadcasted_iota(jnp.int32, (8, rows), 0), 1.0, 0.0
    )
    stacked = jnp.concatenate([marks[:, k * 128 : (k + 1) * 128] for k in range(blocks)], axis=0)
    i0 = lax.broadcasted_iota(jnp.int32, (128, 256), 0)
    i1 = lax.broadcasted_iota(jnp.int32, (128, 256), 1)
    upper = jnp.where((i0 < i1) | (i1 >= 128), 1.0, 0.0).astype(BF16)
    sums = jnp.dot(stacked.astype(BF16), upper, preferred_element_type=F32)
    carry = jnp.zeros((8, 128), F32)
    ranks = []
    for k in range(blocks):
        part = sums[k * 8 : (k + 1) * 8]
        mark = stacked[k * 8 : (k + 1) * 8]
        ranks.append(jnp.sum((part[:, :128] + carry) * mark, axis=0, keepdims=True))
        carry = carry + part[:, 128:]
    rank = jnp.concatenate(ranks, axis=1).astype(jnp.int32)
    q_ref[...] = jnp.where(heading < 4, heading * per + (rank >> 7), -1).astype(F32)
    r_ref[...] = (rank & 127).astype(F32)

    groups = 4 * per
    small_ref[...] = jnp.zeros_like(small_ref)

    def pack(c, carry):
        lanes = pl.ds(pl.multiple_of(c * CHUNK, CHUNK), CHUNK)
        high, low = two_terms(pay_ref[:, lanes])
        both = jnp.concatenate([high.astype(F32), low.astype(F32)], axis=0).astype(BF16)
        q = jnp.broadcast_to(q_ref[:, lanes], (16, CHUNK)).astype(BF16)
        zero = jnp.zeros((16, CHUNK), BF16)
        left = jnp.concatenate([jnp.where(q == float(k), both, zero) for k in range(groups)], axis=0)
        small_ref[...] += dot_nt(left, one_hot_rows(r_ref[:, lanes], 128))
        return carry

    lax.fori_loop(0, rows // CHUNK, pack, 0)
    for h in range(4):
        for j in range(per):
            k = (h * per + j) * 16
            out_bucket[h, :, j * 128 : (j + 1) * 128] = small_ref[k : k + 8, :] + small_ref[k + 8 : k + 16, :]

    pl.semaphore_wait(barrier, n_gx - 1 + n_gy - 1)

    targets = (
        {"gx": lax.rem(gx + n_gx - 1, n_gx)},
        {"gx": lax.rem(gx + 1, n_gx)},
        {"gy": lax.rem(gy + n_gy - 1, n_gy)},
        {"gy": lax.rem(gy + 1, n_gy)},
    )
    landing = (1, 0, 3, 2)

    def exchange(src, dst, send, recv):
        copies = []
        for h in range(4):
            copy = pltpu.make_async_remote_copy(
                src_ref=src.at[h], dst_ref=dst.at[landing[h]], send_sem=send.at[h],
                recv_sem=recv.at[landing[h]], device_id=targets[h], device_id_type=MESH,
            )
            copy.start()
            copies.append(copy)
        return copies

    moves = exchange(out_bucket, in_bucket, bucket_send, bucket_recv)

    cells = cx * cy
    acc_ref[...] = jnp.zeros_like(acc_ref)
    low_ref[...] = jnp.zeros_like(low_ref)

    def build(c, a_ref, b_ref, c_ref, d_ref):
        lanes = pl.ds(pl.multiple_of(c * CHUNK, CHUNK), CHUNK)
        base = (
            jnp.broadcast_to(col_ref[:, lanes], (16, CHUNK))
            - lax.broadcasted_iota(jnp.int32, (16, CHUNK), 0).astype(F32)
        ).astype(BF16)
        zero = jnp.zeros((16, CHUNK), BF16)
        hits = [base == 16.0 * k for k in range(cells // 16)]
        for v in range(5):
            value = jnp.broadcast_to(src_ref[v : v + 1, lanes], (16, CHUNK))
            high, low = two_terms(value)
            low = ((value - high.astype(F32)) * LIFT).astype(BF16)
            for k in range(cells // 16):
                at = v * cells + k * 16
                a_ref[at : at + 16, :] = jnp.where(hits[k], high, zero)
            for k in range(0, cells // 16, 2):
                at = v * cells + k * 16
                pair = jnp.concatenate([jnp.where(hits[k], low, zero), jnp.where(hits[k + 1], low, zero)], axis=0)
                c_ref[at : at + 32, :] = pair.astype(F8)
        depth = one_hot_rows(cell_ref[2:3, lanes].astype(F32), nz)
        b_ref[...] = depth
        d_ref[...] = depth.astype(F8)

    chunks = rows // CHUNK
    build(0, a0_ref, b0_ref, c0_ref, d0_ref)

    def two_chunks(i, carry):
        acc_ref[...] += dot_nt(a0_ref[...], b0_ref[...])
        low_ref[...] += dot_nt(c0_ref[...], d0_ref[...])
        build(2 * i + 1, a1_ref, b1_ref, c1_ref, d1_ref)
        acc_ref[...] += dot_nt(a1_ref[...], b1_ref[...])
        low_ref[...] += dot_nt(c1_ref[...], d1_ref[...])
        build(jnp.minimum(2 * i + 2, chunks - 1), a0_ref, b0_ref, c0_ref, d0_ref)
        return carry

    lax.fori_loop(0, chunks // 2, two_chunks, 0)

    acc_ref[...] += low_ref[...] * (1.0 / LIFT)

    for copy in moves:
        copy.wait_recv()
    for b in range(4):
        got = in_bucket[b]
        state_ref[:, rows + b * cap : rows + (b + 1) * cap] = got[0:5]
        moved_ref[:, rows + b * cap : rows + (b + 1) * cap] = got[5:8].astype(jnp.int32)
        warm = got[4:5]
        share = jax.nn.sigmoid(2.0 * (warm - 2.0))
        boiled = got[0:1] * share / (1.0 - SHRINK * share)
        speed = got[1:4]
        budget = 0.5 * jnp.sum(speed * speed, axis=0, keepdims=True)
        values = [boiled] + [boiled * got[k : k + 1] for k in (1, 2, 3)] + [boiled * (warm + budget)]
        if b < 2:
            along = got[6:7] - (gy * cy).astype(F32)
        else:
            along = got[5:6] - (gx * cx).astype(F32)
        hit = (
            jnp.broadcast_to(along, (16, cap))
            == lax.broadcasted_iota(jnp.int32, (16, cap), 0).astype(F32)
        )
        parts = []
        for value in values:
            wide = jnp.where(hit, jnp.broadcast_to(value, (16, cap)), 0.0)
            parts.append(two_terms(wide))
        left = jnp.concatenate([p[0] for p in parts] + [p[1] for p in parts], axis=0)
        depth = one_hot_rows(got[7:8], nz)
        sums = dot_nt(left, depth)
        sums = sums[0 : 5 * 16] + sums[5 * 16 : 10 * 16]
        for v in range(5):
            part = sums[v * 16 : (v + 1) * 16]
            if b < 2:
                at = v * cells + (0 if b == 0 else (cx - 1) * cy)
                acc_ref[at : at + cy, :] += part
            else:
                edge = 0 if b == 2 else cy - 1
                for x in range(cx):
                    at = v * cells + x * cy + edge
                    acc_ref[at : at + 1, :] += part[x : x + 1]

    def deposit(v):
        return acc_ref[v * cells : (v + 1) * cells, :].reshape(cx, cy, nz)

    for load in loads[4:]:
        load.wait()
    energy = energy_ref[...] + deposit(4)
    en_ref[...] = energy
    pressure = (ADIABATIC_INDEX - 1.0) * energy
    out_face[0] = pressure[0]
    out_face[1] = pressure[cx - 1]
    for x in range(cx):
        out_face[2, x : x + 1, :] = pressure[x, 0:1, :]
        out_face[3, x : x + 1, :] = pressure[x, cy - 1 : cy, :]
    faces = exchange(out_face, in_face, face_send, face_recv)

    density = density_ref[...] + deposit(0)
    rho_ref[...] = density
    lane = lax.broadcasted_iota(jnp.int32, (cx, cy, nz), 2)
    after = jnp.where(lane == nz - 1, 0.0, pltpu.roll(pressure, nz - 1, 2))
    before = jnp.where(lane == 0, 0.0, pltpu.roll(pressure, 1, 2))
    impulse_z = momentum_ref[2] + deposit(3) - KICK * (0.5 * (after - before))
    imp_ref[2] = impulse_z
    sound = jnp.sqrt(ADIABATIC_INDEX * pressure / density)
    for copy in faces:
        copy.wait_recv()
    low_x = jnp.where(gx > 0, in_face[0], 0.0)
    high_x = jnp.where(gx < n_gx - 1, in_face[1], 0.0)
    low_y = jnp.where(gy > 0, in_face[2], 0.0)
    high_y = jnp.where(gy < n_gy - 1, in_face[3], 0.0)
    after = jnp.concatenate([pressure[1:], high_x[None]], axis=0)
    before = jnp.concatenate([low_x[None], pressure[:-1]], axis=0)
    impulse_x = momentum_ref[0] + deposit(1) - KICK * (0.5 * (after - before))
    imp_ref[0] = impulse_x
    line = lax.broadcasted_iota(jnp.int32, (cx, cy, nz), 1)
    after = jnp.where(line == cy - 1, high_y[:, None, :], pltpu.roll(pressure, cy - 1, 1))
    before = jnp.where(line == 0, low_y[:, None, :], pltpu.roll(pressure, 1, 1))
    impulse_y = momentum_ref[1] + deposit(2) - KICK * (0.5 * (after - before))
    imp_ref[1] = impulse_y
    fastest = jnp.maximum(jnp.maximum(jnp.abs(impulse_x), jnp.abs(impulse_y)), jnp.abs(impulse_z))
    wave = fastest / density + sound

    def share_max(value, axis, me, n, slots, send, recv):
        slots[me] = jnp.broadcast_to(value, (8, 128))
        copies = []
        for k in range(1, n):
            copy = pltpu.make_async_remote_copy(
                src_ref=slots.at[me], dst_ref=slots.at[me], send_sem=send.at[k],
                recv_sem=recv.at[k], device_id={axis: lax.rem(me + k, n)}, device_id_type=MESH,
            )
            copy.start()
            copies.append(copy)
        for copy in copies:
            copy.wait_recv()
        best = jnp.max(slots[...])
        return best, copies

    top = jnp.max(jnp.max(wave, axis=(0, 1)))
    top, sent_x = share_max(top, "gx", gx, n_gx, max_x, mx_send, mx_recv)
    top, sent_y = share_max(top, "gy", gy, n_gy, max_y, my_send, my_recv)
    step_ref[...] = COURANT / jnp.broadcast_to(top, (1, 128))
    for copy in moves + faces + sent_x + sent_y:
        copy.wait_send()


def put_out(*refs):
    count = (len(refs) - 1) // 2
    copies = []
    for k in range(count):
        copy = pltpu.make_async_copy(refs[k], refs[count + k], refs[-1].at[k])
        copy.start()
        copies.append(copy)
    for copy in copies:
        copy.wait()


def on_device(n_gx, n_gy, density, momentum, energy, mass, velocity, temp, cell, count):
    rows = mass.shape[0]
    cap = rows // 16
    slots = rows + 4 * cap
    cx, cy, nz = density.shape
    vmem = pl.BlockSpec(memory_space=pltpu.VMEM)
    cells = cx * cy
    outs = pl.pallas_call(
        functools.partial(kernel, n_gx, n_gy),
        out_shape=(
            pltpu.VMEM(density.shape, F32),
            pltpu.VMEM(momentum.shape, F32),
            pltpu.VMEM(energy.shape, F32),
            pltpu.VMEM((5, slots), F32),
            pltpu.VMEM((3, slots), jnp.int32),
            pltpu.VMEM((1, 128), F32),
        ),
        in_specs=[pl.BlockSpec(memory_space=pltpu.SMEM)] + [pl.BlockSpec(memory_space=pltpu.HBM)] * 7,
        out_specs=(vmem,) * 6,
        scratch_shapes=[
            pltpu.VMEM((8, rows), F32),
            pltpu.VMEM((8, rows), F32),
            pltpu.VMEM((1, rows), F32),
            pltpu.VMEM((1, rows), F32),
            pltpu.VMEM((1, rows), F32),
            pltpu.VMEM((5 * cells, CHUNK), BF16),
            pltpu.VMEM((5 * cells, CHUNK), BF16),
            pltpu.VMEM((nz, CHUNK), BF16),
            pltpu.VMEM((nz, CHUNK), BF16),
            pltpu.VMEM((5 * cells, CHUNK), F8),
            pltpu.VMEM((5 * cells, CHUNK), F8),
            pltpu.VMEM((nz, CHUNK), F8),
            pltpu.VMEM((nz, CHUNK), F8),
            pltpu.VMEM((5 * cells, nz), F32),
            pltpu.VMEM((5 * cells, nz), F32),
            pltpu.VMEM((4 * (cap // 128) * 16, 128), F32),
            pltpu.VMEM((4, 8, cap), F32),
            pltpu.VMEM((4, 8, cap), F32),
            pltpu.VMEM((4, cx, nz), F32),
            pltpu.VMEM((4, cx, nz), F32),
            pltpu.VMEM((n_gx, 8, 128), F32),
            pltpu.VMEM((n_gy, 8, 128), F32),
            pltpu.SemaphoreType.DMA((4,)),
            pltpu.SemaphoreType.DMA((4,)),
            pltpu.SemaphoreType.DMA((4,)),
            pltpu.SemaphoreType.DMA((4,)),
            pltpu.SemaphoreType.DMA((n_gx,)),
            pltpu.SemaphoreType.DMA((n_gx,)),
            pltpu.SemaphoreType.DMA((n_gy,)),
            pltpu.SemaphoreType.DMA((n_gy,)),
            pltpu.VMEM(density.shape, F32),
            pltpu.VMEM(momentum.shape, F32),
            pltpu.VMEM(energy.shape, F32),
            pltpu.VMEM((1, rows), F32),
            pltpu.VMEM(velocity.shape, F32),
            pltpu.VMEM((1, rows), F32),
            pltpu.VMEM(cell.shape, jnp.int32),
            pltpu.SemaphoreType.DMA((7,)),
        ],
        compiler_params=pltpu.CompilerParams(
            collective_id=0, has_side_effects=True, vmem_limit_bytes=64200000
        ),
        name="spray",
    )(count, density, momentum, energy, mass.reshape(1, rows), velocity, temp.reshape(1, rows), cell)
    final = pl.pallas_call(
        put_out,
        out_shape=tuple(pltpu.HBM(o.shape, o.dtype) for o in outs[:5]),
        in_specs=[vmem] * 5,
        out_specs=(pl.BlockSpec(memory_space=pltpu.HBM),) * 5,
        scratch_shapes=[pltpu.SemaphoreType.DMA((5,))],
        compiler_params=pltpu.CompilerParams(vmem_limit_bytes=8 * 1024 * 1024),
        name="put_out",
    )(*outs[:5])
    return tuple(final) + (outs[5][0, 0],)


def solution(mesh):
    in_specs = (
        P("gx", "gy", None),
        P(None, "gx", "gy", None),
        P("gx", "gy", None),
        P(("gx", "gy")),
        P(None, ("gx", "gy")),
        P(("gx", "gy")),
        P(None, ("gx", "gy")),
        P(("gx", "gy")),
    )
    out_specs = (
        P("gx", "gy", None),
        P(None, "gx", "gy", None),
        P("gx", "gy", None),
        P(None, ("gx", "gy")),
        P(None, ("gx", "gy")),
        P(),
    )
    return jax.shard_map(
        functools.partial(on_device, mesh.shape["gx"], mesh.shape["gy"]),
        mesh=mesh, in_specs=in_specs, out_specs=out_specs, check_vma=False,
    )
```

profile of v0, /device:TPU:1, one launch (start us, length us, event | category | flops | bytes accessed | tf_op | source)
XLA Modules:
  0.0 46.7 jit_solution(18313191981656713994)
XLA Ops:
  1.3 43.0 %spray.1 = (f32[16,16,256]{2,1,0:T(8,128)S(1)}, f32[3,16,16,256]{3,2,1,0:T(8,128)S(1)}, f32[16,16,256]{2,1,0:T(8,128)S(1)}, f32[5,10240]{1,0:T(8,128)S(1)}, s32[...) custom-call(s32[1]{0:T(128)S(6)} %copy.15.count_ref, f32[16,16,256]{2,1,0:T(8,128)} %density_hbm.1, ...), custom_call_target="tpu_custom_call" | custom-call | tf_op jit(solution)/shard_map/spray/pallas_call | solution.py:323
  44.2 1.3 %put_out.1 = (f32[16,16,256]{2,1,0:T(8,128)}, f32[3,16,16,256]{3,2,1,0:T(8,128)}, f32[16,16,256]{2,1,0:T(8,128)}, f32[5,10240]{1,0:T(8,128)}, s32[3,10240]{1,0:T(4,128)}) custom-call(f32[16,16,256]{2,1,0:T(8,128)S(1)} %get-tuple-element.17.refs_0_, f32[3,16,16,256]{3,2,1,0:T(8,128)S(1)} %get-tuple-element.18.refs_1_, ...), custom_call_target="tpu_custom_call" | custom-call | tf_op jit(solution)/shard_map/put_out/pallas_call | solution.py:380
where the time goes:
time: 46.8 us; the launch traced here: 46.7 us
  Pallas kernels  44.2 us (94%)
  between operations  2.45 us (5%)
    pallas_call x1, Pallas kernels, on_device(): pl.pallas_call(functools.partial(kernel, n_gx, n_gy), out_shape=(pltpu.VM...  43 us
    pallas_call x1, Pallas kernels, on_device(): pl.pallas_call(put_out, out_shape=tuple((pltpu.HBM(o.shape, o.dtype) for...  1.25 us

commit v1 on v0

--- a/solution.py
+++ b/solution.py
@@ -42,17 +42,18 @@
 
 
 def kernel(
-    n_gx, n_gy, count_ref, density_hbm, momentum_hbm, energy_hbm, mass_hbm, vel_hbm, temp_hbm, cell_hbm,
+    n_gx, n_gy, count_hbm, density_hbm, momentum_hbm, energy_hbm, mass_hbm, vel_hbm, temp_hbm, cell_hbm,
     rho_ref, imp_ref, en_ref, state_ref, moved_ref, step_ref,
-    src_ref, pay_ref, col_ref, q_ref, r_ref, a0_ref, a1_ref, b0_ref, b1_ref, c0_ref, c1_ref, d0_ref, d1_ref, acc_ref, low_ref, small_ref,
-    out_bucket, in_bucket, out_face, in_face, max_x, max_y,
-    bucket_send, bucket_recv, face_send, face_recv, mx_send, mx_recv, my_send, my_recv,
-    density_ref, momentum_ref, energy_ref, mass_ref, vel_ref, temp_ref, cell_ref, load_sem,
+    src_ref, pay_ref, col_ref, q_ref, r_ref, a0_ref, a1_ref, c0_ref, c1_ref, e0_ref, e1_ref, f0_ref, f1_ref,
+    b0_ref, b1_ref, d0_ref, d1_ref, acc_ref, low_ref, small_ref,
+    out_bucket, in_bucket, out_face, in_face, max_z, max_p,
+    bucket_send, bucket_recv, face_send, face_recv, mz_send, mz_recv, mp_send, mp_recv,
+    count_ref, density_ref, momentum_ref, energy_ref, mass_ref, vel_ref, temp_ref, cell_ref, load_sem,
 ):
-    sources = (mass_hbm, temp_hbm, vel_hbm, cell_hbm, energy_hbm, density_hbm, momentum_hbm)
-    places = (mass_ref, temp_ref, vel_ref, cell_ref, energy_ref, density_ref, momentum_ref)
+    sources = (count_hbm, mass_hbm, temp_hbm, vel_hbm, cell_hbm, energy_hbm, density_hbm, momentum_hbm)
+    places = (count_ref, mass_ref, temp_ref, vel_ref, cell_ref, energy_ref, density_ref, momentum_ref)
     loads = []
-    for k in range(7):
+    for k in range(8):
         load = pltpu.make_async_copy(sources[k], places[k], load_sem.at[k])
         load.start()
         loads.append(load)
@@ -62,13 +63,31 @@
     cap = rows // 16
     per = cap // 128
 
+    half = n_gy // 2
+    upper_half, plane = gy // half, lax.rem(gy, half)
+    in_column, n_column = upper_half * n_gx + gx, 2 * n_gx
+
+    def column_peer(k):
+        place = lax.rem(in_column + k, n_column)
+        return {"gx": lax.rem(place, n_gx), "gy": place // n_gx * half + plane}
+
+    def plane_peer(k):
+        return {"gy": upper_half * half + lax.rem(plane + k, half)}
+
+    targets = (
+        {"gx": lax.rem(gx + n_gx - 1, n_gx)},
+        {"gx": lax.rem(gx + 1, n_gx)},
+        {"gy": lax.rem(gy + n_gy - 1, n_gy)},
+        {"gy": lax.rem(gy + 1, n_gy)},
+    )
+    landing = (1, 0, 3, 2)
+
     barrier = pltpu.get_barrier_semaphore()
-    for k in range(1, n_gx):
-        pl.semaphore_signal(barrier, inc=1, device_id={"gx": lax.rem(gx + k, n_gx)}, device_id_type=MESH)
-    for k in range(1, n_gy):
-        pl.semaphore_signal(barrier, inc=1, device_id={"gy": lax.rem(gy + k, n_gy)}, device_id_type=MESH)
-
-    for load in loads[:4]:
+    greeted = [column_peer(k) for k in range(1, n_column)] + [plane_peer(k) for k in range(1, half)] + list(targets[2:])
+    for peer in greeted:
+        pl.semaphore_signal(barrier, inc=1, device_id=peer, device_id_type=MESH)
+
+    for load in loads[:5]:
         load.wait()
     mass, temp = mass_ref[...], temp_ref[...]
     live = lax.broadcasted_iota(jnp.int32, (1, rows), 1) < count_ref[0]
@@ -133,16 +152,6 @@
             k = (h * per + j) * 16
             out_bucket[h, :, j * 128 : (j + 1) * 128] = small_ref[k : k + 8, :] + small_ref[k + 8 : k + 16, :]
 
-    pl.semaphore_wait(barrier, n_gx - 1 + n_gy - 1)
-
-    targets = (
-        {"gx": lax.rem(gx + n_gx - 1, n_gx)},
-        {"gx": lax.rem(gx + 1, n_gx)},
-        {"gy": lax.rem(gy + n_gy - 1, n_gy)},
-        {"gy": lax.rem(gy + 1, n_gy)},
-    )
-    landing = (1, 0, 3, 2)
-
     def exchange(src, dst, send, recv):
         copies = []
         for h in range(4):
@@ -154,50 +163,74 @@
             copies.append(copy)
         return copies
 
-    moves = exchange(out_bucket, in_bucket, bucket_send, bucket_recv)
-
     cells = cx * cy
+    chunks = rows // CHUNK
     acc_ref[...] = jnp.zeros_like(acc_ref)
     low_ref[...] = jnp.zeros_like(low_ref)
 
-    def build(c, a_ref, b_ref, c_ref, d_ref):
-        lanes = pl.ds(pl.multiple_of(c * CHUNK, CHUNK), CHUNK)
+    def spread(lanes, values, a_ref, c_ref):
         base = (
             jnp.broadcast_to(col_ref[:, lanes], (16, CHUNK))
             - lax.broadcasted_iota(jnp.int32, (16, CHUNK), 0).astype(F32)
         ).astype(BF16)
         zero = jnp.zeros((16, CHUNK), BF16)
         hits = [base == 16.0 * k for k in range(cells // 16)]
-        for v in range(5):
+        for n, v in enumerate(values):
             value = jnp.broadcast_to(src_ref[v : v + 1, lanes], (16, CHUNK))
-            high, low = two_terms(value)
+            high = value.astype(BF16)
             low = ((value - high.astype(F32)) * LIFT).astype(BF16)
             for k in range(cells // 16):
-                at = v * cells + k * 16
+                at = n * cells + k * 16
                 a_ref[at : at + 16, :] = jnp.where(hits[k], high, zero)
             for k in range(0, cells // 16, 2):
-                at = v * cells + k * 16
+                at = n * cells + k * 16
                 pair = jnp.concatenate([jnp.where(hits[k], low, zero), jnp.where(hits[k + 1], low, zero)], axis=0)
                 c_ref[at : at + 32, :] = pair.astype(F8)
+
+    def chunk_of(c):
+        return pl.ds(pl.multiple_of(c * CHUNK, CHUNK), CHUNK)
+
+    e_rows = slice(4 * cells, 5 * cells)
+
+    def build_energy(c, i, a_ref, c_ref, b_ref, d_ref):
+        lanes, place = chunk_of(c), chunk_of(i)
+        spread(lanes, (4,), a_ref, c_ref)
         depth = one_hot_rows(cell_ref[2:3, lanes].astype(F32), nz)
-        b_ref[...] = depth
-        d_ref[...] = depth.astype(F8)
-
-    chunks = rows // CHUNK
-    build(0, a0_ref, b0_ref, c0_ref, d0_ref)
-
-    def two_chunks(i, carry):
-        acc_ref[...] += dot_nt(a0_ref[...], b0_ref[...])
-        low_ref[...] += dot_nt(c0_ref[...], d0_ref[...])
-        build(2 * i + 1, a1_ref, b1_ref, c1_ref, d1_ref)
-        acc_ref[...] += dot_nt(a1_ref[...], b1_ref[...])
-        low_ref[...] += dot_nt(c1_ref[...], d1_ref[...])
-        build(jnp.minimum(2 * i + 2, chunks - 1), a0_ref, b0_ref, c0_ref, d0_ref)
+        b_ref[:, place] = depth
+        d_ref[:, place] = depth.astype(F8)
+
+    build_energy(0, 0, e0_ref, f0_ref, b0_ref, d0_ref)
+
+    def two_energy(i, carry):
+        place = chunk_of(i)
+        acc_ref[e_rows, :] += dot_nt(e0_ref[...], b0_ref[:, place])
+        low_ref[e_rows, :] += dot_nt(f0_ref[...], d0_ref[:, place])
+        build_energy(2 * i + 1, i, e1_ref, f1_ref, b1_ref, d1_ref)
+        acc_ref[e_rows, :] += dot_nt(e1_ref[...], b1_ref[:, place])
+        low_ref[e_rows, :] += dot_nt(f1_ref[...], d1_ref[:, place])
+        later = jnp.minimum(i + 1, chunks // 2 - 1)
+        build_energy(2 * later, later, e0_ref, f0_ref, b0_ref, d0_ref)
         return carry
 
-    lax.fori_loop(0, chunks // 2, two_chunks, 0)
-
-    acc_ref[...] += low_ref[...] * (1.0 / LIFT)
+    lax.fori_loop(0, chunks // 2, two_energy, 0)
+
+    pl.semaphore_wait(barrier, len(greeted))
+    moves = exchange(out_bucket, in_bucket, bucket_send, bucket_recv)
+
+    others = slice(0, 4 * cells)
+    spread(chunk_of(0), (0, 1, 2, 3), a0_ref, c0_ref)
+
+    def two_others(i, carry):
+        place = chunk_of(i)
+        acc_ref[others, :] += dot_nt(a0_ref[...], b0_ref[:, place])
+        low_ref[others, :] += dot_nt(c0_ref[...], d0_ref[:, place])
+        spread(chunk_of(2 * i + 1), (0, 1, 2, 3), a1_ref, c1_ref)
+        acc_ref[others, :] += dot_nt(a1_ref[...], b1_ref[:, place])
+        low_ref[others, :] += dot_nt(c1_ref[...], d1_ref[:, place])
+        spread(chunk_of(jnp.minimum(2 * i + 2, chunks - 1)), (0, 1, 2, 3), a0_ref, c0_ref)
+        return carry
+
+    lax.fori_loop(0, chunks // 4, two_others, 0)
 
     for copy in moves:
         copy.wait_recv()
@@ -239,20 +272,23 @@
                     acc_ref[at : at + 1, :] += part[x : x + 1]
 
     def deposit(v):
-        return acc_ref[v * cells : (v + 1) * cells, :].reshape(cx, cy, nz)
-
-    for load in loads[4:]:
+        at = slice(v * cells, (v + 1) * cells)
+        return (acc_ref[at, :] + low_ref[at, :] * (1.0 / LIFT)).reshape(cx, cy, nz)
+
+    for load in loads[5:]:
         load.wait()
     energy = energy_ref[...] + deposit(4)
     en_ref[...] = energy
-    pressure = (ADIABATIC_INDEX - 1.0) * energy
-    out_face[0] = pressure[0]
-    out_face[1] = pressure[cx - 1]
+    out_face[0] = (ADIABATIC_INDEX - 1.0) * energy[0]
+    out_face[1] = (ADIABATIC_INDEX - 1.0) * energy[cx - 1]
     for x in range(cx):
-        out_face[2, x : x + 1, :] = pressure[x, 0:1, :]
-        out_face[3, x : x + 1, :] = pressure[x, cy - 1 : cy, :]
+        out_face[2, x : x + 1, :] = (ADIABATIC_INDEX - 1.0) * energy[x, 0:1, :]
+        out_face[3, x : x + 1, :] = (ADIABATIC_INDEX - 1.0) * energy[x, cy - 1 : cy, :]
     faces = exchange(out_face, in_face, face_send, face_recv)
 
+    lax.fori_loop(chunks // 4, chunks // 2, two_others, 0)
+
+    pressure = (ADIABATIC_INDEX - 1.0) * en_ref[...]
     density = density_ref[...] + deposit(0)
     rho_ref[...] = density
     lane = lax.broadcasted_iota(jnp.int32, (cx, cy, nz), 2)
@@ -279,34 +315,37 @@
     fastest = jnp.maximum(jnp.maximum(jnp.abs(impulse_x), jnp.abs(impulse_y)), jnp.abs(impulse_z))
     wave = fastest / density + sound
 
-    def share_max(value, axis, me, n, slots, send, recv):
-        slots[me] = jnp.broadcast_to(value, (8, 128))
+    def share_max(value, me, n, peer, slots, send, recv):
+        slots[me] = value
         copies = []
         for k in range(1, n):
             copy = pltpu.make_async_remote_copy(
                 src_ref=slots.at[me], dst_ref=slots.at[me], send_sem=send.at[k],
-                recv_sem=recv.at[k], device_id={axis: lax.rem(me + k, n)}, device_id_type=MESH,
+                recv_sem=recv.at[k], device_id=peer(k), device_id_type=MESH,
             )
             copy.start()
             copies.append(copy)
         for copy in copies:
             copy.wait_recv()
-        best = jnp.max(slots[...])
-        return best, copies
-
-    top = jnp.max(jnp.max(wave, axis=(0, 1)))
-    top, sent_x = share_max(top, "gx", gx, n_gx, max_x, mx_send, mx_recv)
-    top, sent_y = share_max(top, "gy", gy, n_gy, max_y, my_send, my_recv)
-    step_ref[...] = COURANT / jnp.broadcast_to(top, (1, 128))
-    for copy in moves + faces + sent_x + sent_y:
+        return jnp.max(slots[...], axis=0), copies
+
+    top = jnp.max(jnp.max(wave, axis=0), axis=0, keepdims=True)
+    top = jnp.maximum(top[:, 0:128], top[:, 128:256])
+    top, sent_p = share_max(top, plane, half, plane_peer, max_p, mp_send, mp_recv)
+    top, sent_z = share_max(top, in_column, n_column, column_peer, max_z, mz_send, mz_recv)
+    step_ref[...] = COURANT / jnp.broadcast_to(jnp.max(top), (1, 128))
+    for copy in moves + faces + sent_p + sent_z:
         copy.wait_send()
 
 
 def put_out(*refs):
-    count = (len(refs) - 1) // 2
+    count = (len(refs) - 2) // 2
+    step_ref, sem = refs[-2:]
+    step_ref[0] = refs[count - 1][0, 0]
     copies = []
     for k in range(count):
-        copy = pltpu.make_async_copy(refs[k], refs[count + k], refs[-1].at[k])
+        source = refs[k] if k < count - 1 else step_ref
+        copy = pltpu.make_async_copy(source, refs[count + k], sem.at[k])
         copy.start()
         copies.append(copy)
     for copy in copies:
@@ -319,7 +358,10 @@
     slots = rows + 4 * cap
     cx, cy, nz = density.shape
     vmem = pl.BlockSpec(memory_space=pltpu.VMEM)
+    hbm = pl.BlockSpec(memory_space=pltpu.HBM)
     cells = cx * cy
+    half = n_gy // 2
+    dma = pltpu.SemaphoreType.DMA
     outs = pl.pallas_call(
         functools.partial(kernel, n_gx, n_gy),
         out_shape=(
@@ -330,7 +372,7 @@
             pltpu.VMEM((3, slots), jnp.int32),
             pltpu.VMEM((1, 128), F32),
         ),
-        in_specs=[pl.BlockSpec(memory_space=pltpu.SMEM)] + [pl.BlockSpec(memory_space=pltpu.HBM)] * 7,
+        in_specs=[hbm] * 8,
         out_specs=(vmem,) * 6,
         scratch_shapes=[
             pltpu.VMEM((8, rows), F32),
@@ -338,14 +380,18 @@
             pltpu.VMEM((1, rows), F32),
             pltpu.VMEM((1, rows), F32),
             pltpu.VMEM((1, rows), F32),
-            pltpu.VMEM((5 * cells, CHUNK), BF16),
-            pltpu.VMEM((5 * cells, CHUNK), BF16),
-            pltpu.VMEM((nz, CHUNK), BF16),
-            pltpu.VMEM((nz, CHUNK), BF16),
-            pltpu.VMEM((5 * cells, CHUNK), F8),
-            pltpu.VMEM((5 * cells, CHUNK), F8),
-            pltpu.VMEM((nz, CHUNK), F8),
-            pltpu.VMEM((nz, CHUNK), F8),
+            pltpu.VMEM((4 * cells, CHUNK), BF16),
+            pltpu.VMEM((4 * cells, CHUNK), BF16),
+            pltpu.VMEM((4 * cells, CHUNK), F8),
+            pltpu.VMEM((4 * cells, CHUNK), F8),
+            pltpu.VMEM((cells, CHUNK), BF16),
+            pltpu.VMEM((cells, CHUNK), BF16),
+            pltpu.VMEM((cells, CHUNK), F8),
+            pltpu.VMEM((cells, CHUNK), F8),
+            pltpu.VMEM((nz, rows // 2), BF16),
+            pltpu.VMEM((nz, rows // 2), BF16),
+            pltpu.VMEM((nz, rows // 2), F8),
+            pltpu.VMEM((nz, rows // 2), F8),
             pltpu.VMEM((5 * cells, nz), F32),
             pltpu.VMEM((5 * cells, nz), F32),
             pltpu.VMEM((4 * (cap // 128) * 16, 128), F32),
@@ -353,16 +399,17 @@
             pltpu.VMEM((4, 8, cap), F32),
             pltpu.VMEM((4, cx, nz), F32),
             pltpu.VMEM((4, cx, nz), F32),
-            pltpu.VMEM((n_gx, 8, 128), F32),
-            pltpu.VMEM((n_gy, 8, 128), F32),
-            pltpu.SemaphoreType.DMA((4,)),
-            pltpu.SemaphoreType.DMA((4,)),
-            pltpu.SemaphoreType.DMA((4,)),
-            pltpu.SemaphoreType.DMA((4,)),
-            pltpu.SemaphoreType.DMA((n_gx,)),
-            pltpu.SemaphoreType.DMA((n_gx,)),
-            pltpu.SemaphoreType.DMA((n_gy,)),
-            pltpu.SemaphoreType.DMA((n_gy,)),
+            pltpu.VMEM((2 * n_gx, 1, 128), F32),
+            pltpu.VMEM((half, 1, 128), F32),
+            dma((4,)),
+            dma((4,)),
+            dma((4,)),
+            dma((4,)),
+            dma((2 * n_gx,)),
+            dma((2 * n_gx,)),
+            dma((half,)),
+            dma((half,)),
+            pltpu.SMEM((1,), jnp.int32),
             pltpu.VMEM(density.shape, F32),
             pltpu.VMEM(momentum.shape, F32),
             pltpu.VMEM(energy.shape, F32),
@@ -370,7 +417,7 @@
             pltpu.VMEM(velocity.shape, F32),
             pltpu.VMEM((1, rows), F32),
             pltpu.VMEM(cell.shape, jnp.int32),
-            pltpu.SemaphoreType.DMA((7,)),
+            dma((8,)),
         ],
         compiler_params=pltpu.CompilerParams(
             collective_id=0, has_side_effects=True, vmem_limit_bytes=64200000
@@ -379,14 +426,14 @@
     )(count, density, momentum, energy, mass.reshape(1, rows), velocity, temp.reshape(1, rows), cell)
     final = pl.pallas_call(
         put_out,
-        out_shape=tuple(pltpu.HBM(o.shape, o.dtype) for o in outs[:5]),
-        in_specs=[vmem] * 5,
-        out_specs=(pl.BlockSpec(memory_space=pltpu.HBM),) * 5,
-        scratch_shapes=[pltpu.SemaphoreType.DMA((5,))],
+        out_shape=tuple(pltpu.HBM(o.shape, o.dtype) for o in outs[:5]) + (pltpu.HBM((1,), F32),),
+        in_specs=[vmem] * 6,
+        out_specs=(hbm,) * 6,
+        scratch_shapes=[pltpu.SMEM((1,), F32), dma((6,))],
         compiler_params=pltpu.CompilerParams(vmem_limit_bytes=8 * 1024 * 1024),
         name="put_out",
-    )(*outs[:5])
-    return tuple(final) + (outs[5][0, 0],)
+    )(*outs)
+    return tuple(final[:5]) + (final[5].reshape(()),)
 
 
 def solution(mesh):

time: 46.8 us -> 42.6 us (0.910)
  Pallas kernels: 44.2 us -> 41.2 us
  between operations: 2.45 us -> 1.29 us
    pallas_call x1, Pallas kernels: 43 us -> 39.9 us  [on_device(): pl.pallas_call(functools.partial(kernel, n_gx, n_gy), out_shape=(pltpu.VM...]
where the time goes in v1:
time: 42.6 us; the launch traced here: 42.5 us
  Pallas kernels  41.2 us (97%)
  between operations  1.29 us (3%)
    pallas_call x1, Pallas kernels, on_device(): pl.pallas_call(functools.partial(kernel, n_gx, n_gy), out_shape=(pltpu.VM...  39.9 us
    pallas_call x1, Pallas kernels, on_device(): pl.pallas_call(put_out, out_shape=tuple((pltpu.HBM(o.shape, o.dtype) for...  1.27 us

profile of v1, /device:TPU:1, one launch (start us, length us, event | category | flops | bytes accessed | tf_op | source)
XLA Modules:
  0.0 42.5 jit_solution(11924049096117921669)
XLA Ops:
  1.3 39.9 %spray.1 = (f32[16,16,256]{2,1,0:T(8,128)S(1)}, f32[3,16,16,256]{3,2,1,0:T(8,128)S(1)}, f32[16,16,256]{2,1,0:T(8,128)S(1)}, f32[5,10240]{1,0:T(8,128)S(1)}, s32[...) custom-call(s32[1]{0:T(128)S(6)} %copy.14.count_hbm, f32[16,16,256]{2,1,0:T(8,128)} %density_hbm.1, ...), custom_call_target="tpu_custom_call" | custom-call | tf_op jit(solution)/shard_map/spray/pallas_call | solution.py:365
  41.2 1.3 %put_out.1 = (f32[16,16,256]{2,1,0:T(8,128)}, f32[3,16,16,256]{3,2,1,0:T(8,128)}, f32[16,16,256]{2,1,0:T(8,128)}, f32[5,10240]{1,0:T(8,128)}, s32[3,10240]{1,0:T(4,128)}, /*index=5*/f32[1]{0:T(128)}) custom-call(f32[16,16,256]{2,1,0:T(8,128)S(1)} %get-tuple-element.18.refs_0_, f32[3,16,16,256]{3,2,1,0:T(8,128)S(1)} %get-tuple-element.19.refs_1_, ...), custom_call_target="tpu_custom_call" | custom-call | tf_op jit(solution)/shard_map/put_out/pallas_call | solution.py:427

commit v2 on v1

--- a/solution.py
+++ b/solution.py
@@ -44,7 +44,7 @@
 def kernel(
     n_gx, n_gy, count_hbm, density_hbm, momentum_hbm, energy_hbm, mass_hbm, vel_hbm, temp_hbm, cell_hbm,
     rho_ref, imp_ref, en_ref, state_ref, moved_ref, step_ref,
-    src_ref, pay_ref, col_ref, q_ref, r_ref, a0_ref, a1_ref, c0_ref, c1_ref, e0_ref, e1_ref, f0_ref, f1_ref,
+    src_ref, pay_ref, col_ref, q_ref, r_ref, g0_ref, g1_ref, h0_ref, h1_ref, a0_ref, a1_ref, c0_ref, c1_ref, e0_ref, e1_ref, f0_ref, f1_ref,
     b0_ref, b1_ref, d0_ref, d1_ref, acc_ref, low_ref, small_ref,
     out_bucket, in_bucket, out_face, in_face, max_z, max_p,
     bucket_send, bucket_recv, face_send, face_recv, mz_send, mz_recv, mp_send, mp_recv,
@@ -90,7 +90,7 @@
     for load in loads[:5]:
         load.wait()
     mass, temp = mass_ref[...], temp_ref[...]
-    live = lax.broadcasted_iota(jnp.int32, (1, rows), 1) < count_ref[0]
+    live = lax.broadcasted_iota(jnp.int32, (1, rows), 1) < jnp.broadcast_to(count_ref[...], (1, rows))
     evap = jnp.where(live, mass * jax.nn.sigmoid(2.0 * (temp - 2.0)), 0.0)
     vx, vy, vz = vel_ref[0:1, :], vel_ref[1:2, :], vel_ref[2:3, :]
     src_ref[0:1, :] = evap
@@ -133,24 +133,7 @@
     q_ref[...] = jnp.where(heading < 4, heading * per + (rank >> 7), -1).astype(F32)
     r_ref[...] = (rank & 127).astype(F32)
 
-    groups = 4 * per
-    small_ref[...] = jnp.zeros_like(small_ref)
-
-    def pack(c, carry):
-        lanes = pl.ds(pl.multiple_of(c * CHUNK, CHUNK), CHUNK)
-        high, low = two_terms(pay_ref[:, lanes])
-        both = jnp.concatenate([high.astype(F32), low.astype(F32)], axis=0).astype(BF16)
-        q = jnp.broadcast_to(q_ref[:, lanes], (16, CHUNK)).astype(BF16)
-        zero = jnp.zeros((16, CHUNK), BF16)
-        left = jnp.concatenate([jnp.where(q == float(k), both, zero) for k in range(groups)], axis=0)
-        small_ref[...] += dot_nt(left, one_hot_rows(r_ref[:, lanes], 128))
-        return carry
-
-    lax.fori_loop(0, rows // CHUNK, pack, 0)
-    for h in range(4):
-        for j in range(per):
-            k = (h * per + j) * 16
-            out_bucket[h, :, j * 128 : (j + 1) * 128] = small_ref[k : k + 8, :] + small_ref[k + 8 : k + 16, :]
+    inside = (gx > 0, gx < n_gx - 1, gy > 0, gy < n_gy - 1)
 
     def exchange(src, dst, send, recv):
         copies = []
@@ -159,12 +142,23 @@
                 src_ref=src.at[h], dst_ref=dst.at[landing[h]], send_sem=send.at[h],
                 recv_sem=recv.at[landing[h]], device_id=targets[h], device_id_type=MESH,
             )
-            copy.start()
+            pl.when(inside[h])(copy.start)
             copies.append(copy)
         return copies
 
+    def wait_received(copies):
+        for h in range(4):
+            pl.when(inside[landing[h]])(copies[h].wait_recv)
+
+    for b in range(4):
+        @pl.when(jnp.logical_not(inside[b]))
+        def _():
+            in_bucket[b] = jnp.zeros(in_bucket.shape[1:], F32)
+
     cells = cx * cy
     chunks = rows // CHUNK
+    groups = 4 * per
+    small_ref[...] = jnp.zeros_like(small_ref)
     acc_ref[...] = jnp.zeros_like(acc_ref)
     low_ref[...] = jnp.zeros_like(low_ref)
 
@@ -190,6 +184,16 @@
     def chunk_of(c):
         return pl.ds(pl.multiple_of(c * CHUNK, CHUNK), CHUNK)
 
+    def build_pack(c, g_ref, h_ref):
+        lanes = chunk_of(c)
+        high, low = two_terms(pay_ref[:, lanes])
+        both = jnp.concatenate([high.astype(F32), low.astype(F32)], axis=0).astype(BF16)
+        q = jnp.broadcast_to(q_ref[:, lanes], (16, CHUNK)).astype(BF16)
+        zero = jnp.zeros((16, CHUNK), BF16)
+        for k in range(groups):
+            g_ref[k * 16 : (k + 1) * 16, :] = jnp.where(q == float(k), both, zero)
+        h_ref[...] = one_hot_rows(r_ref[:, lanes], 128)
+
     e_rows = slice(4 * cells, 5 * cells)
 
     def build_energy(c, i, a_ref, c_ref, b_ref, d_ref):
@@ -200,19 +204,29 @@
         d_ref[:, place] = depth.astype(F8)
 
     build_energy(0, 0, e0_ref, f0_ref, b0_ref, d0_ref)
+    build_pack(0, g0_ref, h0_ref)
 
     def two_energy(i, carry):
         place = chunk_of(i)
         acc_ref[e_rows, :] += dot_nt(e0_ref[...], b0_ref[:, place])
         low_ref[e_rows, :] += dot_nt(f0_ref[...], d0_ref[:, place])
+        small_ref[...] += dot_nt(g0_ref[...], h0_ref[...])
         build_energy(2 * i + 1, i, e1_ref, f1_ref, b1_ref, d1_ref)
+        build_pack(2 * i + 1, g1_ref, h1_ref)
         acc_ref[e_rows, :] += dot_nt(e1_ref[...], b1_ref[:, place])
         low_ref[e_rows, :] += dot_nt(f1_ref[...], d1_ref[:, place])
+        small_ref[...] += dot_nt(g1_ref[...], h1_ref[...])
         later = jnp.minimum(i + 1, chunks // 2 - 1)
         build_energy(2 * later, later, e0_ref, f0_ref, b0_ref, d0_ref)
+        build_pack(2 * later, g0_ref, h0_ref)
         return carry
 
     lax.fori_loop(0, chunks // 2, two_energy, 0)
+
+    for h in range(4):
+        for j in range(per):
+            k = (h * per + j) * 16
+            out_bucket[h, :, j * 128 : (j + 1) * 128] = small_ref[k : k + 8, :] + small_ref[k + 8 : k + 16, :]
 
     pl.semaphore_wait(barrier, len(greeted))
     moves = exchange(out_bucket, in_bucket, bucket_send, bucket_recv)
@@ -232,8 +246,7 @@
 
     lax.fori_loop(0, chunks // 4, two_others, 0)
 
-    for copy in moves:
-        copy.wait_recv()
+    wait_received(moves)
     for b in range(4):
         got = in_bucket[b]
         state_ref[:, rows + b * cap : rows + (b + 1) * cap] = got[0:5]
@@ -297,8 +310,7 @@
     impulse_z = momentum_ref[2] + deposit(3) - KICK * (0.5 * (after - before))
     imp_ref[2] = impulse_z
     sound = jnp.sqrt(ADIABATIC_INDEX * pressure / density)
-    for copy in faces:
-        copy.wait_recv()
+    wait_received(faces)
     low_x = jnp.where(gx > 0, in_face[0], 0.0)
     high_x = jnp.where(gx < n_gx - 1, in_face[1], 0.0)
     low_y = jnp.where(gy > 0, in_face[2], 0.0)
@@ -334,7 +346,10 @@
     top, sent_p = share_max(top, plane, half, plane_peer, max_p, mp_send, mp_recv)
     top, sent_z = share_max(top, in_column, n_column, column_peer, max_z, mz_send, mz_recv)
     step_ref[...] = COURANT / jnp.broadcast_to(jnp.max(top), (1, 128))
-    for copy in moves + faces + sent_p + sent_z:
+    for copies in (moves, faces):
+        for h in range(4):
+            pl.when(inside[h])(copies[h].wait_send)
+    for copy in sent_p + sent_z:
         copy.wait_send()
 
 
@@ -380,6 +395,10 @@
             pltpu.VMEM((1, rows), F32),
             pltpu.VMEM((1, rows), F32),
             pltpu.VMEM((1, rows), F32),
+            pltpu.VMEM((4 * (cap // 128) * 16, CHUNK), BF16),
+            pltpu.VMEM((4 * (cap // 128) * 16, CHUNK), BF16),
+            pltpu.VMEM((128, CHUNK), BF16),
+            pltpu.VMEM((128, CHUNK), BF16),
             pltpu.VMEM((4 * cells, CHUNK), BF16),
             pltpu.VMEM((4 * cells, CHUNK), BF16),
             pltpu.VMEM((4 * cells, CHUNK), F8),
@@ -409,7 +428,7 @@
             dma((2 * n_gx,)),
             dma((half,)),
             dma((half,)),
-            pltpu.SMEM((1,), jnp.int32),
+            pltpu.VMEM((1, 1), jnp.int32),
             pltpu.VMEM(density.shape, F32),
             pltpu.VMEM(momentum.shape, F32),
             pltpu.VMEM(energy.shape, F32),
@@ -423,7 +442,7 @@
             collective_id=0, has_side_effects=True, vmem_limit_bytes=64200000
         ),
         name="spray",
-    )(count, density, momentum, energy, mass.reshape(1, rows), velocity, temp.reshape(1, rows), cell)
+    )(count.reshape(1, 1), density, momentum, energy, mass.reshape(1, rows), velocity, temp.reshape(1, rows), cell)
     final = pl.pallas_call(
         put_out,
         out_shape=tuple(pltpu.HBM(o.shape, o.dtype) for o in outs[:5]) + (pltpu.HBM((1,), F32),),

time: 42.6 us -> 38.9 us (0.913)
  Pallas kernels: 41.2 us -> 37.5 us
    pallas_call x1, Pallas kernels: 39.9 us -> 36.2 us  [on_device(): pl.pallas_call(functools.partial(kernel, n_gx, n_gy), out_shape=(pltpu.VM...]
where the time goes in v2:
time: 38.9 us; the launch traced here: 38.8 us
  Pallas kernels  37.5 us (96%)
  between operations  1.29 us (3%)
    pallas_call x1, Pallas kernels, on_device(): pl.pallas_call(functools.partial(kernel, n_gx, n_gy), out_shape=(pltpu.VM...  36.2 us
    pallas_call x1, Pallas kernels, on_device(): pl.pallas_call(put_out, out_shape=tuple((pltpu.HBM(o.shape, o.dtype) for...  1.27 us

profile of v2, /device:TPU:1, one launch (start us, length us, event | category | flops | bytes accessed | tf_op | source)
XLA Modules:
  0.0 38.8 jit_solution(15509793533665283369)
XLA Ops:
  1.3 36.2 %spray.1 = (f32[16,16,256]{2,1,0:T(8,128)S(1)}, f32[3,16,16,256]{3,2,1,0:T(8,128)S(1)}, f32[16,16,256]{2,1,0:T(8,128)S(1)}, f32[5,10240]{1,0:T(8,128)S(1)}, s32[...) custom-call(s32[1,1]{1,0:T(1,128)} %bitcast.4.count_hbm, f32[16,16,256]{2,1,0:T(8,128)} %density_hbm.1, ...), custom_call_target="tpu_custom_call" | custom-call | tf_op jit(solution)/shard_map/spray/pallas_call | solution.py:380
  37.5 1.3 %put_out.1 = (f32[16,16,256]{2,1,0:T(8,128)}, f32[3,16,16,256]{3,2,1,0:T(8,128)}, f32[16,16,256]{2,1,0:T(8,128)}, f32[5,10240]{1,0:T(8,128)}, s32[3,10240]{1,0:T(4,128)}, /*index=5*/f32[1]{0:T(128)}) custom-call(f32[16,16,256]{2,1,0:T(8,128)S(1)} %get-tuple-element.18.refs_0_, f32[3,16,16,256]{3,2,1,0:T(8,128)S(1)} %get-tuple-element.19.refs_1_, ...), custom_call_target="tpu_custom_call" | custom-call | tf_op jit(solution)/shard_map/put_out/pallas_call | solution.py:446

commit v3 on v2

--- a/solution.py
+++ b/solution.py
@@ -17,6 +17,7 @@
 BF16 = jnp.bfloat16
 F8 = jnp.float8_e4m3fn
 LIFT = 2048.0
+SEND_AT = 2
 
 
 def dot_nt(a, b):
@@ -46,7 +47,7 @@
     rho_ref, imp_ref, en_ref, state_ref, moved_ref, step_ref,
     src_ref, pay_ref, col_ref, q_ref, r_ref, g0_ref, g1_ref, h0_ref, h1_ref, a0_ref, a1_ref, c0_ref, c1_ref, e0_ref, e1_ref, f0_ref, f1_ref,
     b0_ref, b1_ref, d0_ref, d1_ref, acc_ref, low_ref, small_ref,
-    out_bucket, in_bucket, out_face, in_face, max_z, max_p,
+    out_bucket, in_bucket, out_face, in_face, own_ref, max_z, max_p,
     bucket_send, bucket_recv, face_send, face_recv, mz_send, mz_recv, mp_send, mp_recv,
     count_ref, density_ref, momentum_ref, energy_ref, mass_ref, vel_ref, temp_ref, cell_ref, load_sem,
 ):
@@ -87,6 +88,8 @@
     for peer in greeted:
         pl.semaphore_signal(barrier, inc=1, device_id=peer, device_id_type=MESH)
 
+    for zeroed in (small_ref, acc_ref, low_ref):
+        zeroed[...] = jnp.zeros_like(zeroed)
     for load in loads[:5]:
         load.wait()
     mass, temp = mass_ref[...], temp_ref[...]
@@ -142,12 +145,15 @@
                 src_ref=src.at[h], dst_ref=dst.at[landing[h]], send_sem=send.at[h],
                 recv_sem=recv.at[landing[h]], device_id=targets[h], device_id_type=MESH,
             )
-            pl.when(inside[h])(copy.start)
             copies.append(copy)
         return copies
 
-    def wait_received(copies):
-        for h in range(4):
+    def send(copies, which):
+        for h in which:
+            pl.when(inside[h])(copies[h].start)
+
+    def wait_received(copies, which):
+        for h in which:
             pl.when(inside[landing[h]])(copies[h].wait_recv)
 
     for b in range(4):
@@ -158,9 +164,6 @@
     cells = cx * cy
     chunks = rows // CHUNK
     groups = 4 * per
-    small_ref[...] = jnp.zeros_like(small_ref)
-    acc_ref[...] = jnp.zeros_like(acc_ref)
-    low_ref[...] = jnp.zeros_like(low_ref)
 
     def spread(lanes, values, a_ref, c_ref):
         base = (
@@ -182,6 +185,8 @@
                 c_ref[at : at + 32, :] = pair.astype(F8)
 
     def chunk_of(c):
+        if isinstance(c, int):
+            return slice(c * CHUNK, (c + 1) * CHUNK)
         return pl.ds(pl.multiple_of(c * CHUNK, CHUNK), CHUNK)
 
     def build_pack(c, g_ref, h_ref):
@@ -194,6 +199,24 @@
             g_ref[k * 16 : (k + 1) * 16, :] = jnp.where(q == float(k), both, zero)
         h_ref[...] = one_hot_rows(r_ref[:, lanes], 128)
 
+    build_pack(0, g0_ref, h0_ref)
+
+    def two_packs(i, carry):
+        small_ref[...] += dot_nt(g0_ref[...], h0_ref[...])
+        build_pack(2 * i + 1, g1_ref, h1_ref)
+        small_ref[...] += dot_nt(g1_ref[...], h1_ref[...])
+        build_pack(jnp.minimum(2 * i + 2, chunks - 1), g0_ref, h0_ref)
+        return carry
+
+    lax.fori_loop(0, chunks // 2, two_packs, 0)
+    for h in range(4):
+        for j in range(per):
+            k = (h * per + j) * 16
+            out_bucket[h, :, j * 128 : (j + 1) * 128] = small_ref[k : k + 8, :] + small_ref[k + 8 : k + 16, :]
+
+    moves = exchange(out_bucket, in_bucket, bucket_send, bucket_recv)
+    faces = exchange(out_face, in_face, face_send, face_recv)
+
     e_rows = slice(4 * cells, 5 * cells)
 
     def build_energy(c, i, a_ref, c_ref, b_ref, d_ref):
@@ -204,59 +227,34 @@
         d_ref[:, place] = depth.astype(F8)
 
     build_energy(0, 0, e0_ref, f0_ref, b0_ref, d0_ref)
-    build_pack(0, g0_ref, h0_ref)
+
+    def send_moves():
+        pl.semaphore_wait(barrier, len(greeted))
+        send(moves, (2, 3, 0, 1))
 
     def two_energy(i, carry):
+        pl.when(i == SEND_AT)(send_moves)
         place = chunk_of(i)
         acc_ref[e_rows, :] += dot_nt(e0_ref[...], b0_ref[:, place])
         low_ref[e_rows, :] += dot_nt(f0_ref[...], d0_ref[:, place])
-        small_ref[...] += dot_nt(g0_ref[...], h0_ref[...])
         build_energy(2 * i + 1, i, e1_ref, f1_ref, b1_ref, d1_ref)
-        build_pack(2 * i + 1, g1_ref, h1_ref)
         acc_ref[e_rows, :] += dot_nt(e1_ref[...], b1_ref[:, place])
         low_ref[e_rows, :] += dot_nt(f1_ref[...], d1_ref[:, place])
-        small_ref[...] += dot_nt(g1_ref[...], h1_ref[...])
         later = jnp.minimum(i + 1, chunks // 2 - 1)
         build_energy(2 * later, later, e0_ref, f0_ref, b0_ref, d0_ref)
-        build_pack(2 * later, g0_ref, h0_ref)
         return carry
 
     lax.fori_loop(0, chunks // 2, two_energy, 0)
 
-    for h in range(4):
-        for j in range(per):
-            k = (h * per + j) * 16
-            out_bucket[h, :, j * 128 : (j + 1) * 128] = small_ref[k : k + 8, :] + small_ref[k + 8 : k + 16, :]
-
-    pl.semaphore_wait(barrier, len(greeted))
-    moves = exchange(out_bucket, in_bucket, bucket_send, bucket_recv)
-
-    others = slice(0, 4 * cells)
-    spread(chunk_of(0), (0, 1, 2, 3), a0_ref, c0_ref)
-
-    def two_others(i, carry):
-        place = chunk_of(i)
-        acc_ref[others, :] += dot_nt(a0_ref[...], b0_ref[:, place])
-        low_ref[others, :] += dot_nt(c0_ref[...], d0_ref[:, place])
-        spread(chunk_of(2 * i + 1), (0, 1, 2, 3), a1_ref, c1_ref)
-        acc_ref[others, :] += dot_nt(a1_ref[...], b1_ref[:, place])
-        low_ref[others, :] += dot_nt(c1_ref[...], d1_ref[:, place])
-        spread(chunk_of(jnp.minimum(2 * i + 2, chunks - 1)), (0, 1, 2, 3), a0_ref, c0_ref)
-        return carry
-
-    lax.fori_loop(0, chunks // 4, two_others, 0)
-
-    wait_received(moves)
-    for b in range(4):
-        got = in_bucket[b]
-        state_ref[:, rows + b * cap : rows + (b + 1) * cap] = got[0:5]
-        moved_ref[:, rows + b * cap : rows + (b + 1) * cap] = got[5:8].astype(jnp.int32)
+    def sums_of(got, b, with_all):
         warm = got[4:5]
         share = jax.nn.sigmoid(2.0 * (warm - 2.0))
         boiled = got[0:1] * share / (1.0 - SHRINK * share)
         speed = got[1:4]
         budget = 0.5 * jnp.sum(speed * speed, axis=0, keepdims=True)
-        values = [boiled] + [boiled * got[k : k + 1] for k in (1, 2, 3)] + [boiled * (warm + budget)]
+        values = [boiled * (warm + budget)]
+        if with_all:
+            values = [boiled] + [boiled * got[k : k + 1] for k in (1, 2, 3)] + values
         if b < 2:
             along = got[6:7] - (gy * cy).astype(F32)
         else:
@@ -270,9 +268,15 @@
             wide = jnp.where(hit, jnp.broadcast_to(value, (16, cap)), 0.0)
             parts.append(two_terms(wide))
         left = jnp.concatenate([p[0] for p in parts] + [p[1] for p in parts], axis=0)
-        depth = one_hot_rows(got[7:8], nz)
-        sums = dot_nt(left, depth)
-        sums = sums[0 : 5 * 16] + sums[5 * 16 : 10 * 16]
+        sums = dot_nt(left, one_hot_rows(got[7:8], nz))
+        n = len(values) * 16
+        return sums[0:n] + sums[n : 2 * n]
+
+    def receive(b):
+        got = in_bucket[b]
+        state_ref[:, rows + b * cap : rows + (b + 1) * cap] = got[0:5]
+        moved_ref[:, rows + b * cap : rows + (b + 1) * cap] = got[5:8].astype(jnp.int32)
+        sums = sums_of(got, b, True)
         for v in range(5):
             part = sums[v * 16 : (v + 1) * 16]
             if b < 2:
@@ -288,18 +292,46 @@
         at = slice(v * cells, (v + 1) * cells)
         return (acc_ref[at, :] + low_ref[at, :] * (1.0 / LIFT)).reshape(cx, cy, nz)
 
-    for load in loads[5:]:
-        load.wait()
-    energy = energy_ref[...] + deposit(4)
-    en_ref[...] = energy
-    out_face[0] = (ADIABATIC_INDEX - 1.0) * energy[0]
-    out_face[1] = (ADIABATIC_INDEX - 1.0) * energy[cx - 1]
-    for x in range(cx):
-        out_face[2, x : x + 1, :] = (ADIABATIC_INDEX - 1.0) * energy[x, 0:1, :]
-        out_face[3, x : x + 1, :] = (ADIABATIC_INDEX - 1.0) * energy[x, cy - 1 : cy, :]
-    faces = exchange(out_face, in_face, face_send, face_recv)
-
-    lax.fori_loop(chunks // 4, chunks // 2, two_others, 0)
+    def receive_x():
+        wait_received(moves, (0, 1))
+        receive(0)
+        receive(1)
+        for load in loads[5:]:
+            load.wait()
+        energy = energy_ref[...] + deposit(4)
+        for x in range(cx):
+            out_face[2, x : x + 1, :] = (ADIABATIC_INDEX - 1.0) * energy[x, 0:1, :]
+            out_face[3, x : x + 1, :] = (ADIABATIC_INDEX - 1.0) * energy[x, cy - 1 : cy, :]
+        send(faces, (2, 3))
+
+    def receive_y():
+        wait_received(moves, (2, 3))
+        receive(2)
+        receive(3)
+        for h in (2, 3):
+            own_ref[h - 2] = (ADIABATIC_INDEX - 1.0) * sums_of(out_bucket[h], h, False)
+        energy = energy_ref[...] + deposit(4)
+        en_ref[...] = energy
+        out_face[0] = (ADIABATIC_INDEX - 1.0) * energy[0]
+        out_face[1] = (ADIABATIC_INDEX - 1.0) * energy[cx - 1]
+        send(faces, (0, 1))
+
+    others = slice(0, 4 * cells)
+    spread(chunk_of(0), (0, 1, 2, 3), a0_ref, c0_ref)
+
+    def two_others(i, carry):
+        pl.when(i == 1)(receive_x)
+        pl.when(i == 2)(receive_y)
+        place = chunk_of(i)
+        acc_ref[others, :] += dot_nt(a0_ref[...], b0_ref[:, place])
+        low_ref[others, :] += dot_nt(c0_ref[...], d0_ref[:, place])
+        spread(chunk_of(2 * i + 1), (0, 1, 2, 3), a1_ref, c1_ref)
+        acc_ref[others, :] += dot_nt(a1_ref[...], b1_ref[:, place])
+        low_ref[others, :] += dot_nt(c1_ref[...], d1_ref[:, place])
+        spread(chunk_of(jnp.minimum(2 * i + 2, chunks - 1)), (0, 1, 2, 3), a0_ref, c0_ref)
+        return carry
+
+    lax.fori_loop(0, chunks // 2, two_others, 0)
 
     pressure = (ADIABATIC_INDEX - 1.0) * en_ref[...]
     density = density_ref[...] + deposit(0)
@@ -310,11 +342,11 @@
     impulse_z = momentum_ref[2] + deposit(3) - KICK * (0.5 * (after - before))
     imp_ref[2] = impulse_z
     sound = jnp.sqrt(ADIABATIC_INDEX * pressure / density)
-    wait_received(faces)
+    wait_received(faces, range(4))
     low_x = jnp.where(gx > 0, in_face[0], 0.0)
     high_x = jnp.where(gx < n_gx - 1, in_face[1], 0.0)
-    low_y = jnp.where(gy > 0, in_face[2], 0.0)
-    high_y = jnp.where(gy < n_gy - 1, in_face[3], 0.0)
+    low_y = jnp.where(gy > 0, in_face[2] + own_ref[0], 0.0)
+    high_y = jnp.where(gy < n_gy - 1, in_face[3] + own_ref[1], 0.0)
     after = jnp.concatenate([pressure[1:], high_x[None]], axis=0)
     before = jnp.concatenate([low_x[None], pressure[:-1]], axis=0)
     impulse_x = momentum_ref[0] + deposit(1) - KICK * (0.5 * (after - before))
@@ -418,6 +450,7 @@
             pltpu.VMEM((4, 8, cap), F32),
             pltpu.VMEM((4, cx, nz), F32),
             pltpu.VMEM((4, cx, nz), F32),
+            pltpu.VMEM((2, cx, nz), F32),
             pltpu.VMEM((2 * n_gx, 1, 128), F32),
             pltpu.VMEM((half, 1, 128), F32),
             dma((4,)),

time: 38.9 us -> 36.7 us (0.943)
  Pallas kernels: 37.5 us -> 35.3 us
    pallas_call x1, Pallas kernels: 36.2 us -> 34.1 us  [on_device(): pl.pallas_call(functools.partial(kernel, n_gx, n_gy), out_shape=(pltpu.VM...]
where the time goes in v3:
time: 36.7 us; the launch traced here: 36.6 us
  Pallas kernels  35.3 us (96%)
  between operations  1.29 us (4%)
    pallas_call x1, Pallas kernels, on_device(): pl.pallas_call(functools.partial(kernel, n_gx, n_gy), out_shape=(pltpu.VM...  34.1 us
    pallas_call x1, Pallas kernels, on_device(): pl.pallas_call(put_out, out_shape=tuple((pltpu.HBM(o.shape, o.dtype) for...  1.27 us

profile of v3, /device:TPU:1, one launch (start us, length us, event | category | flops | bytes accessed | tf_op | source)
XLA Modules:
  0.0 36.6 jit_solution(7445664935134537591)
XLA Ops:
  1.3 34.1 %spray.1 = (f32[16,16,256]{2,1,0:T(8,128)S(1)}, f32[3,16,16,256]{3,2,1,0:T(8,128)S(1)}, f32[16,16,256]{2,1,0:T(8,128)S(1)}, f32[5,10240]{1,0:T(8,128)S(1)}, s32[...) custom-call(s32[1,1]{1,0:T(1,128)} %bitcast.4.count_hbm, f32[16,16,256]{2,1,0:T(8,128)} %density_hbm.1, ...), custom_call_target="tpu_custom_call" | custom-call | tf_op jit(solution)/shard_map/spray/pallas_call | solution.py:412
  35.3 1.3 %put_out.1 = (f32[16,16,256]{2,1,0:T(8,128)}, f32[3,16,16,256]{3,2,1,0:T(8,128)}, f32[16,16,256]{2,1,0:T(8,128)}, f32[5,10240]{1,0:T(8,128)}, s32[3,10240]{1,0:T(4,128)}, /*index=5*/f32[1]{0:T(128)}) custom-call(f32[16,16,256]{2,1,0:T(8,128)S(1)} %get-tuple-element.18.refs_0_, f32[3,16,16,256]{3,2,1,0:T(8,128)S(1)} %get-tuple-element.19.refs_1_, ...), custom_call_target="tpu_custom_call" | custom-call | tf_op jit(solution)/shard_map/put_out/pallas_call | solution.py:479

commit v4 on v3

--- a/solution.py
+++ b/solution.py
@@ -18,6 +18,7 @@
 F8 = jnp.float8_e4m3fn
 LIFT = 2048.0
 SEND_AT = 2
+HUB_GX, HUB_GY = 1, 0
 
 
 def dot_nt(a, b):
@@ -47,8 +48,8 @@
     rho_ref, imp_ref, en_ref, state_ref, moved_ref, step_ref,
     src_ref, pay_ref, col_ref, q_ref, r_ref, g0_ref, g1_ref, h0_ref, h1_ref, a0_ref, a1_ref, c0_ref, c1_ref, e0_ref, e1_ref, f0_ref, f1_ref,
     b0_ref, b1_ref, d0_ref, d1_ref, acc_ref, low_ref, small_ref,
-    out_bucket, in_bucket, out_face, in_face, own_ref, max_z, max_p,
-    bucket_send, bucket_recv, face_send, face_recv, mz_send, mz_recv, mp_send, mp_recv,
+    out_bucket, in_bucket, out_face, in_face, own_ref, max_z, max_p, max_h,
+    bucket_send, bucket_recv, face_send, face_recv, mz_send, mz_recv, mp_send, mp_recv, mh_send, mh_recv,
     count_ref, density_ref, momentum_ref, energy_ref, mass_ref, vel_ref, temp_ref, cell_ref, load_sem,
 ):
     sources = (count_hbm, mass_hbm, temp_hbm, vel_hbm, cell_hbm, energy_hbm, density_hbm, momentum_hbm)
@@ -87,6 +88,22 @@
     greeted = [column_peer(k) for k in range(1, n_column)] + [plane_peer(k) for k in range(1, half)] + list(targets[2:])
     for peer in greeted:
         pl.semaphore_signal(barrier, inc=1, device_id=peer, device_id_type=MESH)
+
+    devices = n_gx * n_gy
+    is_hub = (gx == HUB_GX) & (gy == HUB_GY)
+    not_hub = jnp.logical_not(is_hub)
+    hub = HUB_GY * n_gx + HUB_GX
+    hub_slot = lax.rem(gy * n_gx + gx + devices - hub - 1, devices)
+
+    @pl.when(is_hub)
+    def _():
+        def greet(k, carry):
+            other = lax.rem(k + hub + 1, devices)
+            peer = {"gx": lax.rem(other, n_gx), "gy": other // n_gx}
+            pl.semaphore_signal(barrier, inc=1, device_id=peer, device_id_type=MESH)
+            return carry
+
+        lax.fori_loop(0, devices - 1, greet, 0)
 
     for zeroed in (small_ref, acc_ref, low_ref):
         zeroed[...] = jnp.zeros_like(zeroed)
@@ -229,7 +246,8 @@
     build_energy(0, 0, e0_ref, f0_ref, b0_ref, d0_ref)
 
     def send_moves():
-        pl.semaphore_wait(barrier, len(greeted))
+        pl.when(is_hub)(lambda: pl.semaphore_wait(barrier, len(greeted)))
+        pl.when(not_hub)(lambda: pl.semaphore_wait(barrier, len(greeted) + 1))
         send(moves, (2, 3, 0, 1))
 
     def two_energy(i, carry):
@@ -359,29 +377,59 @@
     fastest = jnp.maximum(jnp.maximum(jnp.abs(impulse_x), jnp.abs(impulse_y)), jnp.abs(impulse_z))
     wave = fastest / density + sound
 
-    def share_max(value, me, n, peer, slots, send, recv):
-        slots[me] = value
+    def share_max(me, n, peer, slots, send, recv):
         copies = []
         for k in range(1, n):
-            copy = pltpu.make_async_remote_copy(
+            copies.append(pltpu.make_async_remote_copy(
                 src_ref=slots.at[me], dst_ref=slots.at[me], send_sem=send.at[k],
                 recv_sem=recv.at[k], device_id=peer(k), device_id_type=MESH,
-            )
-            copy.start()
-            copies.append(copy)
-        for copy in copies:
+            ))
+        return copies
+
+    top = jnp.max(jnp.max(wave, axis=0), axis=0, keepdims=True)
+    max_p[plane] = jnp.maximum(top[:, 0:128], top[:, 128:256])
+    to_hub = pltpu.make_async_remote_copy(
+        src_ref=max_p.at[plane], dst_ref=max_h.at[hub_slot], send_sem=mh_send.at[0],
+        recv_sem=mh_recv.at[0], device_id={"gx": HUB_GX, "gy": HUB_GY}, device_id_type=MESH,
+    )
+    pl.when(not_hub)(to_hub.start)
+    sent_p = share_max(plane, half, plane_peer, max_p, mp_send, mp_recv)
+    for copy in sent_p:
+        copy.start()
+    for copy in sent_p:
+        copy.wait_recv()
+    max_z[in_column] = jnp.max(max_p[...], axis=0)
+    sent_z = share_max(in_column, n_column, column_peer, max_z, mz_send, mz_recv)
+    for k in range(1, n_column):
+        peer = column_peer(k)
+        to_other = jnp.logical_not((peer["gx"] == HUB_GX) & (peer["gy"] == HUB_GY))
+        pl.when(to_other)(sent_z[k - 1].start)
+
+    @pl.when(not_hub)
+    def _():
+        for copy in sent_z:
             copy.wait_recv()
-        return jnp.max(slots[...], axis=0), copies
-
-    top = jnp.max(jnp.max(wave, axis=0), axis=0, keepdims=True)
-    top = jnp.maximum(top[:, 0:128], top[:, 128:256])
-    top, sent_p = share_max(top, plane, half, plane_peer, max_p, mp_send, mp_recv)
-    top, sent_z = share_max(top, in_column, n_column, column_peer, max_z, mz_send, mz_recv)
-    step_ref[...] = COURANT / jnp.broadcast_to(jnp.max(top), (1, 128))
+        step_ref[...] = COURANT / jnp.broadcast_to(jnp.max(max_z[...]), (1, 128))
+
+    @pl.when(is_hub)
+    def _():
+        arrived = max_h.at[pl.ds(0, devices - 1)]
+        pltpu.make_async_remote_copy(
+            src_ref=arrived, dst_ref=arrived, send_sem=mh_send.at[0], recv_sem=mh_recv.at[0],
+            device_id={"gx": HUB_GX, "gy": HUB_GY}, device_id_type=MESH,
+        ).wait_recv()
+        best = jnp.maximum(jnp.max(arrived[...], axis=0), max_p[plane])
+        step_ref[...] = COURANT / jnp.broadcast_to(jnp.max(best), (1, 128))
+
+    pl.when(not_hub)(to_hub.wait_send)
+    for k in range(1, n_column):
+        peer = column_peer(k)
+        to_other = jnp.logical_not((peer["gx"] == HUB_GX) & (peer["gy"] == HUB_GY))
+        pl.when(to_other)(sent_z[k - 1].wait_send)
     for copies in (moves, faces):
         for h in range(4):
             pl.when(inside[h])(copies[h].wait_send)
-    for copy in sent_p + sent_z:
+    for copy in sent_p:
         copy.wait_send()
 
 
@@ -453,6 +501,7 @@
             pltpu.VMEM((2, cx, nz), F32),
             pltpu.VMEM((2 * n_gx, 1, 128), F32),
             pltpu.VMEM((half, 1, 128), F32),
+            pltpu.VMEM((n_gx * n_gy, 1, 128), F32),
             dma((4,)),
             dma((4,)),
             dma((4,)),
@@ -461,6 +510,8 @@
             dma((2 * n_gx,)),
             dma((half,)),
             dma((half,)),
+            dma((1,)),
+            dma((1,)),
             pltpu.VMEM((1, 1), jnp.int32),
             pltpu.VMEM(density.shape, F32),
             pltpu.VMEM(momentum.shape, F32),

time: 36.7 us -> 35.1 us (0.956); the launches traced: 36.6 us -> 34.5 us
  Pallas kernels: 35.3 us -> 33.2 us
    pallas_call x1, Pallas kernels: 34.1 us -> 32 us  [on_device(): pl.pallas_call(functools.partial(kernel, n_gx, n_gy), out_shape=(pltpu.VM...]
where the time goes in v4:
time: 35.1 us; the launch traced here: 34.5 us
  Pallas kernels  33.2 us (95%)
  between operations  1.29 us (4%)
    pallas_call x1, Pallas kernels, on_device(): pl.pallas_call(functools.partial(kernel, n_gx, n_gy), out_shape=(pltpu.VM...  32 us
    pallas_call x1, Pallas kernels, on_device(): pl.pallas_call(put_out, out_shape=tuple((pltpu.HBM(o.shape, o.dtype) for...  1.27 us

profile of v4, /device:TPU:1, one launch (start us, length us, event | category | flops | bytes accessed | tf_op | source)
XLA Modules:
  0.0 34.5 jit_solution(2560717386693637539)
XLA Ops:
  1.3 32.0 %spray.1 = (f32[16,16,256]{2,1,0:T(8,128)S(1)}, f32[3,16,16,256]{3,2,1,0:T(8,128)S(1)}, f32[16,16,256]{2,1,0:T(8,128)S(1)}, f32[5,10240]{1,0:T(8,128)S(1)}, s32[...) custom-call(s32[1,1]{1,0:T(1,128)} %bitcast.4.count_hbm, f32[16,16,256]{2,1,0:T(8,128)} %density_hbm.1, ...), custom_call_target="tpu_custom_call" | custom-call | tf_op jit(solution)/shard_map/spray/pallas_call | solution.py:460
  33.2 1.3 %put_out.1 = (f32[16,16,256]{2,1,0:T(8,128)}, f32[3,16,16,256]{3,2,1,0:T(8,128)}, f32[16,16,256]{2,1,0:T(8,128)}, f32[5,10240]{1,0:T(8,128)}, s32[3,10240]{1,0:T(4,128)}, /*index=5*/f32[1]{0:T(128)}) custom-call(f32[16,16,256]{2,1,0:T(8,128)S(1)} %get-tuple-element.18.refs_0_, f32[3,16,16,256]{3,2,1,0:T(8,128)S(1)} %get-tuple-element.19.refs_1_, ...), custom_call_target="tpu_custom_call" | custom-call | tf_op jit(solution)/shard_map/put_out/pallas_call | solution.py:530

commit v5 on v4

--- a/solution.py
+++ b/solution.py
@@ -17,8 +17,7 @@
 BF16 = jnp.bfloat16
 F8 = jnp.float8_e4m3fn
 LIFT = 2048.0
-SEND_AT = 2
-HUB_GX, HUB_GY = 1, 0
+HUBS = ((1, 0), (0, 1), (1, 1), (0, 4), (1, 4), (2, 0), (3, 0))
 
 
 def dot_nt(a, b):
@@ -90,20 +89,27 @@
         pl.semaphore_signal(barrier, inc=1, device_id=peer, device_id_type=MESH)
 
     devices = n_gx * n_gy
-    is_hub = (gx == HUB_GX) & (gy == HUB_GY)
+
+    def is_at(place, spots):
+        found = jnp.bool_(False)
+        for spot in spots:
+            found = found | ((place[0] == spot[0]) & (place[1] == spot[1]))
+        return found
+
+    is_hub = is_at((gx, gy), HUBS)
     not_hub = jnp.logical_not(is_hub)
-    hub = HUB_GY * n_gx + HUB_GX
-    hub_slot = lax.rem(gy * n_gx + gx + devices - hub - 1, devices)
+    me = gy * n_gx + gx
 
     @pl.when(is_hub)
     def _():
-        def greet(k, carry):
-            other = lax.rem(k + hub + 1, devices)
-            peer = {"gx": lax.rem(other, n_gx), "gy": other // n_gx}
-            pl.semaphore_signal(barrier, inc=1, device_id=peer, device_id_type=MESH)
+        def greet(j, carry):
+            for k in range(15):
+                other = lax.rem(j * 15 + k + me + 1, devices)
+                peer = {"gx": lax.rem(other, n_gx), "gy": other // n_gx}
+                pl.semaphore_signal(barrier, inc=1, device_id=peer, device_id_type=MESH)
             return carry
 
-        lax.fori_loop(0, devices - 1, greet, 0)
+        lax.fori_loop(0, (devices - 1) // 15, greet, 0)
 
     for zeroed in (small_ref, acc_ref, low_ref):
         zeroed[...] = jnp.zeros_like(zeroed)
@@ -218,19 +224,6 @@
 
     build_pack(0, g0_ref, h0_ref)
 
-    def two_packs(i, carry):
-        small_ref[...] += dot_nt(g0_ref[...], h0_ref[...])
-        build_pack(2 * i + 1, g1_ref, h1_ref)
-        small_ref[...] += dot_nt(g1_ref[...], h1_ref[...])
-        build_pack(jnp.minimum(2 * i + 2, chunks - 1), g0_ref, h0_ref)
-        return carry
-
-    lax.fori_loop(0, chunks // 2, two_packs, 0)
-    for h in range(4):
-        for j in range(per):
-            k = (h * per + j) * 16
-            out_bucket[h, :, j * 128 : (j + 1) * 128] = small_ref[k : k + 8, :] + small_ref[k + 8 : k + 16, :]
-
     moves = exchange(out_bucket, in_bucket, bucket_send, bucket_recv)
     faces = exchange(out_face, in_face, face_send, face_recv)
 
@@ -246,23 +239,31 @@
     build_energy(0, 0, e0_ref, f0_ref, b0_ref, d0_ref)
 
     def send_moves():
-        pl.when(is_hub)(lambda: pl.semaphore_wait(barrier, len(greeted)))
-        pl.when(not_hub)(lambda: pl.semaphore_wait(barrier, len(greeted) + 1))
+        pl.when(is_hub)(lambda: pl.semaphore_wait(barrier, len(greeted) + len(HUBS) - 1))
+        pl.when(not_hub)(lambda: pl.semaphore_wait(barrier, len(greeted) + len(HUBS)))
         send(moves, (2, 3, 0, 1))
 
     def two_energy(i, carry):
-        pl.when(i == SEND_AT)(send_moves)
         place = chunk_of(i)
         acc_ref[e_rows, :] += dot_nt(e0_ref[...], b0_ref[:, place])
         low_ref[e_rows, :] += dot_nt(f0_ref[...], d0_ref[:, place])
+        small_ref[...] += dot_nt(g0_ref[...], h0_ref[...])
         build_energy(2 * i + 1, i, e1_ref, f1_ref, b1_ref, d1_ref)
+        build_pack(2 * i + 1, g1_ref, h1_ref)
         acc_ref[e_rows, :] += dot_nt(e1_ref[...], b1_ref[:, place])
         low_ref[e_rows, :] += dot_nt(f1_ref[...], d1_ref[:, place])
+        small_ref[...] += dot_nt(g1_ref[...], h1_ref[...])
         later = jnp.minimum(i + 1, chunks // 2 - 1)
         build_energy(2 * later, later, e0_ref, f0_ref, b0_ref, d0_ref)
+        build_pack(2 * later, g0_ref, h0_ref)
         return carry
 
     lax.fori_loop(0, chunks // 2, two_energy, 0)
+    for h in range(4):
+        for j in range(per):
+            k = (h * per + j) * 16
+            out_bucket[h, :, j * 128 : (j + 1) * 128] = small_ref[k : k + 8, :] + small_ref[k + 8 : k + 16, :]
+    send_moves()
 
     def sums_of(got, b, with_all):
         warm = got[4:5]
@@ -339,7 +340,7 @@
 
     def two_others(i, carry):
         pl.when(i == 1)(receive_x)
-        pl.when(i == 2)(receive_y)
+        pl.when(i == 3)(receive_y)
         place = chunk_of(i)
         acc_ref[others, :] += dot_nt(a0_ref[...], b0_ref[:, place])
         low_ref[others, :] += dot_nt(c0_ref[...], d0_ref[:, place])
@@ -388,11 +389,15 @@
 
     top = jnp.max(jnp.max(wave, axis=0), axis=0, keepdims=True)
     max_p[plane] = jnp.maximum(top[:, 0:128], top[:, 128:256])
-    to_hub = pltpu.make_async_remote_copy(
-        src_ref=max_p.at[plane], dst_ref=max_h.at[hub_slot], send_sem=mh_send.at[0],
-        recv_sem=mh_recv.at[0], device_id={"gx": HUB_GX, "gy": HUB_GY}, device_id_type=MESH,
-    )
-    pl.when(not_hub)(to_hub.start)
+    to_hubs = []
+    for n, spot in enumerate(HUBS):
+        hub = spot[1] * n_gx + spot[0]
+        to_hubs.append((jnp.logical_not(is_at((gx, gy), (spot,))), pltpu.make_async_remote_copy(
+            src_ref=max_p.at[plane], dst_ref=max_h.at[lax.rem(me + devices - hub - 1, devices)], send_sem=mh_send.at[n],
+            recv_sem=mh_recv.at[0], device_id={"gx": spot[0], "gy": spot[1]}, device_id_type=MESH,
+        )))
+    for other, copy in to_hubs:
+        pl.when(other)(copy.start)
     sent_p = share_max(plane, half, plane_peer, max_p, mp_send, mp_recv)
     for copy in sent_p:
         copy.start()
@@ -402,7 +407,7 @@
     sent_z = share_max(in_column, n_column, column_peer, max_z, mz_send, mz_recv)
     for k in range(1, n_column):
         peer = column_peer(k)
-        to_other = jnp.logical_not((peer["gx"] == HUB_GX) & (peer["gy"] == HUB_GY))
+        to_other = jnp.logical_not(is_at((peer["gx"], peer["gy"]), HUBS))
         pl.when(to_other)(sent_z[k - 1].start)
 
     @pl.when(not_hub)
@@ -416,15 +421,16 @@
         arrived = max_h.at[pl.ds(0, devices - 1)]
         pltpu.make_async_remote_copy(
             src_ref=arrived, dst_ref=arrived, send_sem=mh_send.at[0], recv_sem=mh_recv.at[0],
-            device_id={"gx": HUB_GX, "gy": HUB_GY}, device_id_type=MESH,
+            device_id={"gx": HUBS[0][0], "gy": HUBS[0][1]}, device_id_type=MESH,
         ).wait_recv()
         best = jnp.maximum(jnp.max(arrived[...], axis=0), max_p[plane])
         step_ref[...] = COURANT / jnp.broadcast_to(jnp.max(best), (1, 128))
 
-    pl.when(not_hub)(to_hub.wait_send)
+    for other, copy in to_hubs:
+        pl.when(other)(copy.wait_send)
     for k in range(1, n_column):
         peer = column_peer(k)
-        to_other = jnp.logical_not((peer["gx"] == HUB_GX) & (peer["gy"] == HUB_GY))
+        to_other = jnp.logical_not(is_at((peer["gx"], peer["gy"]), HUBS))
         pl.when(to_other)(sent_z[k - 1].wait_send)
     for copies in (moves, faces):
         for h in range(4):
@@ -510,7 +516,7 @@
             dma((2 * n_gx,)),
             dma((half,)),
             dma((half,)),
-            dma((1,)),
+            dma((len(HUBS),)),
             dma((1,)),
             pltpu.VMEM((1, 1), jnp.int32),
             pltpu.VMEM(density.shape, F32),

time: 35.1 us -> 34.2 us (0.974); the launches traced: 34.5 us -> 34 us
  Pallas kernels: 33.2 us -> 32.8 us
    pallas_call x1, Pallas kernels: 32 us -> 31.5 us  [on_device(): pl.pallas_call(functools.partial(kernel, n_gx, n_gy), out_shape=(pltpu.VM...]
where the time goes in v5:
time: 34.2 us; the launch traced here: 34 us
  Pallas kernels  32.8 us (96%)
  between operations  1.29 us (4%)
    pallas_call x1, Pallas kernels, on_device(): pl.pallas_call(functools.partial(kernel, n_gx, n_gy), out_shape=(pltpu.VM...  31.5 us
    pallas_call x1, Pallas kernels, on_device(): pl.pallas_call(put_out, out_shape=tuple((pltpu.HBM(o.shape, o.dtype) for...  1.27 us

profile of v5, /device:TPU:1, one launch (start us, length us, event | category | flops | bytes accessed | tf_op | source)
XLA Modules:
  0.0 34.0 jit_solution(7019762280497375498)
XLA Ops:
  1.3 31.5 %spray.1 = (f32[16,16,256]{2,1,0:T(8,128)S(1)}, f32[3,16,16,256]{3,2,1,0:T(8,128)S(1)}, f32[16,16,256]{2,1,0:T(8,128)S(1)}, f32[5,10240]{1,0:T(8,128)S(1)}, s32[...) custom-call(s32[1,1]{1,0:T(1,128)} %bitcast.4.count_hbm, f32[16,16,256]{2,1,0:T(8,128)} %density_hbm.1, ...), custom_call_target="tpu_custom_call" | custom-call | tf_op jit(solution)/shard_map/spray/pallas_call | solution.py:466
  32.8 1.3 %put_out.1 = (f32[16,16,256]{2,1,0:T(8,128)}, f32[3,16,16,256]{3,2,1,0:T(8,128)}, f32[16,16,256]{2,1,0:T(8,128)}, f32[5,10240]{1,0:T(8,128)}, s32[3,10240]{1,0:T(4,128)}, /*index=5*/f32[1]{0:T(128)}) custom-call(f32[16,16,256]{2,1,0:T(8,128)S(1)} %get-tuple-element.18.refs_0_, f32[3,16,16,256]{3,2,1,0:T(8,128)S(1)} %get-tuple-element.19.refs_1_, ...), custom_call_target="tpu_custom_call" | custom-call | tf_op jit(solution)/shard_map/put_out/pallas_call | solution.py:536

commit v6 on v5

--- a/solution.py
+++ b/solution.py
@@ -258,7 +258,7 @@
         build_pack(2 * later, g0_ref, h0_ref)
         return carry
 
-    lax.fori_loop(0, chunks // 2, two_energy, 0)
+    lax.fori_loop(0, chunks // 4, lambda i, carry: two_energy(2 * i + 1, two_energy(2 * i, carry)), 0)
     for h in range(4):
         for j in range(per):
             k = (h * per + j) * 16
@@ -335,12 +335,13 @@
         out_face[1] = (ADIABATIC_INDEX - 1.0) * energy[cx - 1]
         send(faces, (0, 1))
 
+    far = (gy == half - 1) | (gy == half)
     others = slice(0, 4 * cells)
     spread(chunk_of(0), (0, 1, 2, 3), a0_ref, c0_ref)
 
     def two_others(i, carry):
         pl.when(i == 1)(receive_x)
-        pl.when(i == 3)(receive_y)
+        pl.when(((i == 2) & jnp.logical_not(far)) | ((i == 3) & far))(receive_y)
         place = chunk_of(i)
         acc_ref[others, :] += dot_nt(a0_ref[...], b0_ref[:, place])
         low_ref[others, :] += dot_nt(c0_ref[...], d0_ref[:, place])

time: 34.2 us -> 34 us (level)
  no operation moved by 1% of the time
where the time goes in v6:
time: 34 us; the launch traced here: 33.9 us
  Pallas kernels  32.6 us (96%)
  between operations  1.29 us (4%)
    pallas_call x1, Pallas kernels, on_device(): pl.pallas_call(functools.partial(kernel, n_gx, n_gy), out_shape=(pltpu.VM...  31.4 us
    pallas_call x1, Pallas kernels, on_device(): pl.pallas_call(put_out, out_shape=tuple((pltpu.HBM(o.shape, o.dtype) for...  1.27 us

profile of v6, /device:TPU:1, one launch (start us, length us, event | category | flops | bytes accessed | tf_op | source)
XLA Modules:
  0.0 33.9 jit_solution(4568992351291609074)
XLA Ops:
  1.3 31.4 %spray.1 = (f32[16,16,256]{2,1,0:T(8,128)S(1)}, f32[3,16,16,256]{3,2,1,0:T(8,128)S(1)}, f32[16,16,256]{2,1,0:T(8,128)S(1)}, f32[5,10240]{1,0:T(8,128)S(1)}, s32[...) custom-call(s32[1,1]{1,0:T(1,128)} %bitcast.4.count_hbm, f32[16,16,256]{2,1,0:T(8,128)} %density_hbm.1, ...), custom_call_target="tpu_custom_call" | custom-call | tf_op jit(solution)/shard_map/spray/pallas_call | solution.py:467
  32.7 1.3 %put_out.1 = (f32[16,16,256]{2,1,0:T(8,128)}, f32[3,16,16,256]{3,2,1,0:T(8,128)}, f32[16,16,256]{2,1,0:T(8,128)}, f32[5,10240]{1,0:T(8,128)}, s32[3,10240]{1,0:T(4,128)}, /*index=5*/f32[1]{0:T(128)}) custom-call(f32[16,16,256]{2,1,0:T(8,128)S(1)} %get-tuple-element.18.refs_0_, f32[3,16,16,256]{3,2,1,0:T(8,128)S(1)} %get-tuple-element.19.refs_1_, ...), custom_call_target="tpu_custom_call" | custom-call | tf_op jit(solution)/shard_map/put_out/pallas_call | solution.py:537

commit v7 on v6

--- a/solution.py
+++ b/solution.py
@@ -136,8 +136,6 @@
     heading = jnp.where(live, heading, 5)
     stays = heading == 4
     col_ref[...] = jnp.where(stays, lx * cy + ly, -1000).astype(F32)
-    state_ref[:, :rows] = jnp.where(stays, pay_ref[0:5, :], 0.0)
-    moved_ref[:, :rows] = jnp.where(stays, cell_ref[...], 0)
 
     blocks = rows // 128
     marks = jnp.where(
@@ -293,8 +291,6 @@
 
     def receive(b):
         got = in_bucket[b]
-        state_ref[:, rows + b * cap : rows + (b + 1) * cap] = got[0:5]
-        moved_ref[:, rows + b * cap : rows + (b + 1) * cap] = got[5:8].astype(jnp.int32)
         sums = sums_of(got, b, True)
         for v in range(5):
             part = sums[v * 16 : (v + 1) * 16]
@@ -402,6 +398,12 @@
     sent_p = share_max(plane, half, plane_peer, max_p, mp_send, mp_recv)
     for copy in sent_p:
         copy.start()
+    stays = col_ref[...] >= 0.0
+    state_ref[:, :rows] = jnp.where(stays, pay_ref[0:5, :], 0.0)
+    moved_ref[:, :rows] = jnp.where(stays, cell_ref[...], 0)
+    for b in range(4):
+        state_ref[:, rows + b * cap : rows + (b + 1) * cap] = in_bucket[b, 0:5]
+        moved_ref[:, rows + b * cap : rows + (b + 1) * cap] = in_bucket[b, 5:8].astype(jnp.int32)
     for copy in sent_p:
         copy.wait_recv()
     max_z[in_column] = jnp.max(max_p[...], axis=0)

time: 34 us -> 33.9 us (level)
  no operation moved by 1% of the time
where the time goes in v7:
time: 33.9 us; the launch traced here: 33.8 us
  Pallas kernels  32.5 us (96%)
  between operations  1.29 us (4%)
    pallas_call x1, Pallas kernels, on_device(): pl.pallas_call(functools.partial(kernel, n_gx, n_gy), out_shape=(pltpu.VM...  31.3 us
    pallas_call x1, Pallas kernels, on_device(): pl.pallas_call(put_out, out_shape=tuple((pltpu.HBM(o.shape, o.dtype) for...  1.27 us

profile of v7, /device:TPU:1, one launch (start us, length us, event | category | flops | bytes accessed | tf_op | source)
XLA Modules:
  0.0 33.8 jit_solution(7225219049713787145)
XLA Ops:
  1.3 31.3 %spray.1 = (f32[16,16,256]{2,1,0:T(8,128)S(1)}, f32[3,16,16,256]{3,2,1,0:T(8,128)S(1)}, f32[16,16,256]{2,1,0:T(8,128)S(1)}, f32[5,10240]{1,0:T(8,128)S(1)}, s32[...) custom-call(s32[1,1]{1,0:T(1,128)} %bitcast.4.count_hbm, f32[16,16,256]{2,1,0:T(8,128)} %density_hbm.1, ...), custom_call_target="tpu_custom_call" | custom-call | tf_op jit(solution)/shard_map/spray/pallas_call | solution.py:469
  32.6 1.3 %put_out.1 = (f32[16,16,256]{2,1,0:T(8,128)}, f32[3,16,16,256]{3,2,1,0:T(8,128)}, f32[16,16,256]{2,1,0:T(8,128)}, f32[5,10240]{1,0:T(8,128)}, s32[3,10240]{1,0:T(4,128)}, /*index=5*/f32[1]{0:T(128)}) custom-call(f32[16,16,256]{2,1,0:T(8,128)S(1)} %get-tuple-element.18.refs_0_, f32[3,16,16,256]{3,2,1,0:T(8,128)S(1)} %get-tuple-element.19.refs_1_, ...), custom_call_target="tpu_custom_call" | custom-call | tf_op jit(solution)/shard_map/put_out/pallas_call | solution.py:539
